TPU v7x, 32 devices: a whole 2x2x4 slice. The times are simulated.
32 devices in a mesh: seq: 8 (over z, core), dp: 4 (over y, x).
Axes of the slice: x: 2, y: 2, z: 4, core: 2. Of those that a mesh axis runs over, the one named last changes fastest.
Arguments:
- block_input: bfloat16 [4, 1024, 4096], P('dp', 'seq'), may hold values from -8 to 8
- cotangent: bfloat16 [4, 1024, 4096], P('dp', 'seq'), may hold values from -6 to 6
- pool_weight: float32 [4, 4, 4096], P(None, None, 'dp'), may hold values from 0.1 to 0.6
Outputs:
- input_grad: bfloat16 [4, 1024, 4096], P('dp', 'seq')
- weight_grad: float32 [4, 4, 4096], P(None, None, 'dp')
All inputs are finite; a program needn't handle non-finite values.
Results may differ from a plain program's by a relative error of at most 0.009.
Values may be sent and summed in bfloat16 or wider, within the bound.
No kernel may reach another device: no remote copies, remote signals or barrier semaphores. Data moves between devices by JAX's collectives and lax.ppermute only.
A program may use at most 64 MiB of HBM per device.

v0:
```python
import functools

import jax
import jax.numpy as jnp
from jax import lax
from jax.experimental import pallas as pl
from jax.experimental.pallas import tpu as pltpu
from jax.sharding import PartitionSpec as P


HEAD_DIM = 128
POOL = 4
KINDS = 4
CHUNKS = 2
BF16 = jnp.bfloat16
F32 = jnp.float32


VMEM = pl.BlockSpec(memory_space=pltpu.VMEM)
ANY = pl.BlockSpec(memory_space=pl.ANY)


def dot(a, b, ca, cb):
    return lax.dot_general(a, b, (((ca,), (cb,)), ((), ())), preferred_element_type=F32)


def messages(n):
    return [*range(n // 2, n), *range(2, n // 2), 1]


def send(block, axis, n, message):
    return lax.ppermute(block, axis, [(s, s ^ message) for s in range(n)])


def places(n):
    me = lax.axis_index("seq")
    return [me] + [lax.bitwise_xor(me, jnp.int32(m)) for m in messages(n)]


def interleave_matrix(rows):
    r = lax.broadcasted_iota(jnp.int32, (rows, rows), 0)
    t = lax.broadcasted_iota(jnp.int32, (rows, rows), 1)
    hit = t == POOL * r
    for j in range(1, POOL):
        hit = hit | (t - j == POOL * r - j * rows)
    return jnp.where(hit, 1.0, 0.0).astype(BF16)


def aligned(index, size):
    return pl.ds(pl.multiple_of(index * size, size), size)


def cut_kernel(n, wide, first, which, x_ref, y_ref, *refs):
    outs, sem = refs[:-1], refs[-1]
    rows = x_ref.shape[0]
    cw = outs[0].shape[1]
    copies = []
    goal = [places(n)[i] for i in which]
    for i in range(len(which)):
        cols = pl.ds(pl.multiple_of(goal[i] * wide + first, HEAD_DIM), cw)
        for t, ref in enumerate((x_ref, y_ref)):
            copy = pltpu.make_async_copy(ref.at[:, cols], outs[i].at[t * rows : (t + 1) * rows, :], sem.at[2 * i + t])
            copy.start()
            copies.append(copy)
    for copy in copies:
        copy.wait()


def block_kernel(n, nd, rc, wide, first, weight, *refs):
    blocks = refs[:n]
    outs = refs[n : 2 * n]
    q_ref, k_ref, v_ref, x_ref, y_ref, g_ref, a_ref, qg, kg, vg, wg_ref = refs[2 * n :]
    length, width = q_ref.shape
    rows = rc * POOL
    place = places(n)
    goal = place
    me, col, share = lax.axis_index("seq"), lax.axis_index("dp"), n // nd
    w = weight[
        lax.bitwise_xor(col, lax.div(me, share)),
        :,
        pl.ds(pl.multiple_of(lax.rem(me, share) * wide + first, HEAD_DIM), width),
    ]
    sel = interleave_matrix(rows)
    for i in range(n):
        at = aligned(place[i], rc)
        x = dot(sel, blocks[i][:rows, :], 1, 0)
        y = dot(sel, blocks[i][rows:, :], 1, 0)
        for j in range(POOL):
            x_ref[j, at, :] = x[j * rc : (j + 1) * rc].astype(BF16)
            y_ref[j, at, :] = y[j * rc : (j + 1) * rc].astype(BF16)
        for t, (ref, src) in enumerate(((q_ref, x), (k_ref, x), (v_ref, x), (g_ref, y))):
            total = src[:rc] * w[t * POOL][None, :]
            for j in range(1, POOL):
                total = total + src[j * rc : (j + 1) * rc] * w[t * POOL + j][None, :]
            ref[at, :] = total.astype(BF16).astype(ref.dtype)
    g_ref[length:, :] = jnp.zeros((8, width), F32)
    g_ref[:length, :] = g_ref[1 : length + 1, :]
    a_ref[:8, :] = jnp.zeros((8, width), F32)
    scale = HEAD_DIM**-0.5
    step = min(length, 256)
    many = length > step
    if many:
        kg[...] = jnp.zeros_like(kg)
        vg[...] = jnp.zeros_like(vg)
    for h in range(width // HEAD_DIM):
        cols = slice(h * HEAD_DIM, (h + 1) * HEAD_DIM)

        def body(start):
            at = pl.ds(start, step)
            q, k, v = q_ref[at, cols], k_ref[:, cols], v_ref[:, cols]
            s = dot(q, k, 1, 1) * scale
            qi = lax.broadcasted_iota(jnp.int32, s.shape, 0) + start
            ki = lax.broadcasted_iota(jnp.int32, s.shape, 1)
            s = jnp.where(qi >= ki, s, -1e30)
            e = jnp.exp(s - jnp.max(s, -1, keepdims=True))
            p = e * (1.0 / jnp.sum(e, -1, keepdims=True))
            p_low = p.astype(BF16)
            attended = dot(p_low, v, 1, 0)
            later = g_ref[at, cols]
            low = later.astype(BF16)
            delta = jnp.sum(later * attended, -1, keepdims=True)
            sg = (p * (dot(low, v, 1, 1) - delta)).astype(BF16)
            a_ref[pl.ds(start + 8, step), cols] = attended
            qg[at, cols] = (dot(sg, k, 1, 0) * scale).astype(BF16).astype(F32)
            new_k = dot(sg, q, 0, 0) * scale
            new_v = dot(p_low, low, 0, 0)
            if many:
                kg[:, cols] += new_k
                vg[:, cols] += new_v
            else:
                kg[:, cols] = new_k.astype(BF16).astype(F32)
                vg[:, cols] = new_v.astype(BF16).astype(F32)

        if many:

            def run(i, carry):
                body(pl.multiple_of(i * step, step))
                return carry

            lax.fori_loop(0, length // step, run, 0)
        else:
            body(0)
    if many:
        kg[...] = kg[...].astype(BF16).astype(F32)
        vg[...] = vg[...].astype(BF16).astype(F32)
    for t, ref in enumerate((qg, kg, vg)):
        for i in range(n):
            outs[i][t * rc : (t + 1) * rc, :] = ref[aligned(goal[i], rc), :].astype(BF16)
        for j in range(POOL):
            wg_ref[t * POOL + j, :] = jnp.sum(ref[...] * x_ref[j].astype(F32), 0)
    shifted = a_ref[7 : length + 7, :].astype(BF16).astype(F32)
    for j in range(POOL):
        wg_ref[3 * POOL + j, :] = jnp.sum(shifted * y_ref[j].astype(F32), 0)
    low = wg_ref[...].astype(BF16)
    for i in range(n):
        outs[i][3 * rc :, :] = low


def collect_kernel(n, nd, wide, *refs):
    blocks, outs, held = refs[: -nd - 1], refs[-nd - 1 : -1], refs[-1]
    place, col, share = places(n), lax.axis_index("dp"), n // nd
    cw = blocks[0].shape[1]
    for c in range(len(blocks) // n):
        for i in range(n):
            part = blocks[c * n + i][...].astype(F32)
            cols = pl.ds(pl.multiple_of(lax.rem(place[i], share) * wide + c * cw, HEAD_DIM), cw)
            for t in range(KINDS):
                held[lax.div(place[i], share), t, :, cols] = part[t * POOL : (t + 1) * POOL]
    for k in range(nd):
        outs[k][...] = held[lax.bitwise_xor(col, jnp.int32(k))]


def spread_kernel(n, nd, wide, weight, *refs):
    blocks, out = refs[:-1], refs[-1]
    place, col, share = places(n), lax.axis_index("dp"), n // nd
    rc = out.shape[0] // POOL
    cw = blocks[0].shape[1]
    sel = interleave_matrix(rc * POOL)
    for c in range(len(blocks) // n):
        for i in range(n):
            ref = blocks[c * n + i]
            cols = pl.ds(pl.multiple_of(place[i] * wide + c * cw, HEAD_DIM), cw)
            w = weight[
                lax.bitwise_xor(col, lax.div(place[i], share)),
                :,
                pl.ds(pl.multiple_of(lax.rem(place[i], share) * wide + c * cw, HEAD_DIM), cw),
            ]
            parts = [ref[t * rc : (t + 1) * rc, :].astype(F32) for t in range(3)]
            made = []
            for j in range(POOL):
                total = parts[0] * w[j][None, :]
                for t in range(1, 3):
                    total = total + parts[t] * w[t * POOL + j][None, :]
                made.append(total.astype(BF16))
            out[:, cols] = dot(sel, jnp.concatenate(made, 0), 0, 0).astype(BF16)


def per_device(n, nd, block_input, cotangent, pool_weight):
    inputs = block_input[0]
    upstream = cotangent[0]
    rows, width = inputs.shape
    wide = width // n
    rc = rows // POOL
    length = rc * n
    heads = wide // HEAD_DIM
    chunks = CHUNKS if heads % CHUNKS == 0 else 1
    cw = wide // chunks
    todo = messages(n)
    shape = jax.ShapeDtypeStruct

    arrived = []
    for c in range(chunks):
        cut = [None] * n
        groups = [range(1, 1 + n // 2), [0, *range(1 + n // 2, n)]] if c == 0 else [range(n)]
        for part, which in enumerate(groups):
            made = pl.pallas_call(
                functools.partial(cut_kernel, n, wide, c * cw, which),
                out_shape=[shape((2 * rows, cw), BF16)] * len(which),
                in_specs=[ANY, ANY],
                out_specs=[VMEM] * len(which),
                scratch_shapes=[pltpu.SemaphoreType.DMA((2 * len(which),))],
            )(inputs, upstream)
            for i, block in zip(which, made):
                cut[i] = block
        got = [cut[0]]
        for b, m in zip(cut[1:], todo):
            got.append(send(b, "seq", n, m))
        arrived.append(got)
    own = pool_weight.reshape(KINDS * POOL, -1)
    pieces = [own] + [send(own, "dp", nd, k) for k in range(1, nd)]
    weights = jnp.stack(pieces)

    back = []
    for c in range(chunks):
        full = lambda kind: pltpu.VMEM((length, cw), kind)
        made = pl.pallas_call(
            functools.partial(block_kernel, n, nd, rc, wide, c * cw),
            out_shape=[shape((3 * rc + KINDS * POOL, cw), BF16)] * n,
            in_specs=[VMEM] * (1 + n),
            out_specs=[VMEM] * n,
            scratch_shapes=[full(BF16)] * 3
            + [pltpu.VMEM((POOL, length, cw), BF16)] * 2
            + [pltpu.VMEM((length + 8, cw), F32)] * 2
            + [full(F32)] * 3
            + [pltpu.VMEM((KINDS * POOL, cw), F32)],
        )(weights, *arrived[c])
        back.append(made[0])
        for b, m in zip(made[1:], todo):
            back.append(send(b, "seq", n, m))

    tail = pl.BlockSpec((KINDS * POOL, cw), lambda i: (3 * rc // (KINDS * POOL), 0))
    owned = (KINDS, POOL, width // nd)
    part = pl.BlockSpec(owned, lambda i: (0, 0, 0))
    shares = pl.pallas_call(
        functools.partial(collect_kernel, n, nd, wide),
        out_shape=[shape(owned, F32)] * nd,
        grid=(1,),
        in_specs=[tail] * len(back),
        out_specs=[part] * nd,
        scratch_shapes=[pltpu.VMEM((nd,) + owned, F32)],
    )(*back)
    weight_grad = shares[0]
    for k in range(1, nd):
        weight_grad = weight_grad + send(shares[k], "dp", nd, k)
    input_grad = pl.pallas_call(
        functools.partial(spread_kernel, n, nd, wide),
        out_shape=shape((rows, width), BF16),
        in_specs=[VMEM] * (1 + len(back)),
        out_specs=VMEM,
    )(weights, *back)
    return input_grad[None], weight_grad


def solution(mesh):
    n, nd = mesh.shape["seq"], mesh.shape["dp"]
    if n < 4 or n & (n - 1) or n % nd:
        raise ValueError("unsupported mesh")
    placed = (P("dp", "seq", None), P("dp", "seq", None), P(None, None, "dp"))

    def whole_step(*arrays):
        return per_device(n, nd, *arrays)

    return jax.shard_map(
        whole_step,
        mesh=mesh,
        in_specs=placed,
        out_specs=(P("dp", "seq", None), P(None, None, "dp")),
        check_vma=False,
    )
```

profile of v0, /device:TPU:0, one launch (start us, length us, event | category | flops | bytes accessed | tf_op | source)
XLA Modules:
  0.0 92.9 jit_solution(14555997514126821166)
XLA Ops:
  0.6 0.9 reshape.7
  1.5 4.0 %collective-permute-start.2 = (f32[16,1024]{1,0:T(8,128)S(1)}, f32[16,1024]{1,0:T(8,128)S(1)}, u32[]{:S(2)}, u32[]{:S(2)}) collective-permute-start(f32[16,1024]{1,0:T(8,128)S(1)} %reshape.7), channel_id=1, source_target_pairs={{0,3},{1,2},{2,1},{3,0},{4,7},{5,6},{6,5},{7,4},{8,11},{9,10},{10,... | collective-permute-start | bytes 196616 | tf_op jit(solution)/shard_map/ppermute | solution.py:32
  5.5 0.5 collective-permute-start.1
  6.0 1.9 %shard_map.51 = (bf16[256,256]{1,0:T(8,128)(2,1)}, bf16[256,256]{1,0:T(8,128)(2,1)}, bf16[256,256]{1,0:T(8,128)(2,1)}, bf16[256,256]{1,0:T(8,128)(2,1)}) custom-call(bf16[128,4096]{1,0:T(8,128)(2,1)} %bitcast.11, bf16[128,4096]{1,0:T(8,128)(2,1)} %bitcast.14), custom_call_target="tpu_custom_call" | custom-call | tf_op jit(solution)/shard_map/pallas_call | solution.py:216
  7.9 2.7 %collective-permute-start.3 = (bf16[256,256]{1,0:T(8,128)(2,1)}, bf16[256,256]{1,0:T(8,128)(2,1)S(1)}, u32[]{:S(2)}, u32[]{:S(2)}) collective-permute-start(bf16[256,256]{1,0:T(8,128)(2,1)} %get-tuple-element.39), channel_id=1, source_target_pairs={{0,16},{4,20},{8,24},{12,28},{16,0},{20,4},{24,8},{28,12},{1,17},{... | collective-permute-start | bytes 393224 | tf_op jit(solution)/shard_map/ppermute | solution.py:32
  10.6 2.5 %collective-permute-start.5 = (bf16[256,256]{1,0:T(8,128)(2,1)}, bf16[256,256]{1,0:T(8,128)(2,1)S(1)}, u32[]{:S(2)}, u32[]{:S(2)}) collective-permute-start(bf16[256,256]{1,0:T(8,128)(2,1)} %get-tuple-element.41), channel_id=1, source_target_pairs={{0,24},{4,28},{8,16},{12,20},{16,8},{20,12},{24,0},{28,4},{1,25},{... | collective-permute-start | bytes 393224 | tf_op jit(solution)/shard_map/ppermute | solution.py:32
  13.1 1.1 %collective-permute-start.6 = (bf16[256,256]{1,0:T(8,128)(2,1)}, bf16[256,256]{1,0:T(8,128)(2,1)S(1)}, u32[]{:S(2)}, u32[]{:S(2)}) collective-permute-start(bf16[256,256]{1,0:T(8,128)(2,1)} %get-tuple-element.42), channel_id=1, source_target_pairs={{0,28},{4,24},{8,20},{12,16},{16,12},{20,8},{24,4},{28,0},{1,29},{... | collective-permute-start | bytes 393224 | tf_op jit(solution)/shard_map/ppermute | solution.py:32
  14.3 0.0 collective-permute-done.1
  14.3 0.5 collective-permute-start
  14.8 1.9 %shard_map.50 = (bf16[256,256]{1,0:T(8,128)(2,1)}, bf16[256,256]{1,0:T(8,128)(2,1)}, bf16[256,256]{1,0:T(8,128)(2,1)}, bf16[256,256]{1,0:T(8,128)(2,1)}) custom-call(bf16[128,4096]{1,0:T(8,128)(2,1)} %bitcast.12, bf16[128,4096]{1,0:T(8,128)(2,1)} %bitcast.15), custom_call_target="tpu_custom_call" | custom-call | tf_op jit(solution)/shard_map/pallas_call | solution.py:216
  16.7 0.0 copy-start
  16.8 2.5 %shard_map.53 = (bf16[256,256]{1,0:T(8,128)(2,1)}, bf16[256,256]{1,0:T(8,128)(2,1)}, bf16[256,256]{1,0:T(8,128)(2,1)}, bf16[256,256]{1,0:T(8,128)(2,1)}, bf16[25...) custom-call(bf16[128,4096]{1,0:T(8,128)(2,1)} %bitcast.13, ...), custom_call_target="tpu_custom_call" | custom-call | tf_op jit(solution)/shard_map/pallas_call | solution.py:216
  19.2 0.0 collective-permute-done
  19.3 0.1 collective-permute-start.7
  19.3 6.9 %collective-permute-done.3.refs_1_ = bf16[256,256]{1,0:T(8,128)(2,1)S(1)} collective-permute-done((bf16[256,256]{1,0:T(8,128)(2,1)}, bf16[256,256]{1,0:T(8,128)(2,1)S(1)}, u32[]{:S(2)}, u32[]{:S(2)}) %collective-permute-start.3) | collective-permute-done | bytes 131104 | tf_op jit(solution)/shard_map/ppermute | solution.py:32
  26.2 0.6 collective-permute-done.4.refs_2_
  26.8 2.0 %collective-permute-start.9 = (bf16[256,256]{1,0:T(8,128)(2,1)S(1)}, bf16[256,256]{1,0:T(8,128)(2,1)S(1)}, u32[]{:S(2)}, u32[]{:S(2)}) collective-permute-start(bf16[256,256]{1,0:T(8,128)(2,1)S(1)} %copy-done.31), channel_id=1, source_target_pairs={{0,4},{4,0},{8,12},{12,8},{16,20},{20,16},{24,28},{28,24},{1,5},{5... | collective-permute-start | bytes 393224 | tf_op jit(solution)/shard_map/ppermute | solution.py:32
  28.8 4.6 %collective-permute-start.17 = (bf16[256,256]{1,0:T(8,128)(2,1)}, bf16[256,256]{1,0:T(8,128)(2,1)S(1)}, u32[]{:S(2)}, u32[]{:S(2)}) collective-permute-start(bf16[256,256]{1,0:T(8,128)(2,1)} %get-tuple-element.55), channel_id=1, source_target_pairs={{0,16},{4,20},{8,24},{12,28},{16,0},{20,4},{24,8},{28,12},{1,17},{... | collective-permute-start | bytes 393224 | tf_op jit(solution)/shard_map/ppermute | solution.py:32
  33.4 0.0 collective-permute-done.6.refs_4_
  33.4 2.3 %collective-permute-start.18 = (bf16[256,256]{1,0:T(8,128)(2,1)}, bf16[256,256]{1,0:T(8,128)(2,1)S(1)}, u32[]{:S(2)}, u32[]{:S(2)}) collective-permute-start(bf16[256,256]{1,0:T(8,128)(2,1)} %get-tuple-element.56), channel_id=1, source_target_pairs={{0,20},{4,16},{8,28},{12,24},{16,4},{20,0},{24,12},{28,8},{1,21},{... | collective-permute-start | bytes 393224 | tf_op jit(solution)/shard_map/ppermute | solution.py:32
  35.7 0.0 collective-permute-done.7.refs_5_
  35.7 0.6 collective-permute-start.19
  36.3 3.0 %collective-permute-start.20 = (bf16[256,256]{1,0:T(8,128)(2,1)}, bf16[256,256]{1,0:T(8,128)(2,1)S(1)}, u32[]{:S(2)}, u32[]{:S(2)}) collective-permute-start(bf16[256,256]{1,0:T(8,128)(2,1)} %get-tuple-element.58), channel_id=1, source_target_pairs={{0,28},{4,24},{8,20},{12,16},{16,12},{20,8},{24,4},{28,0},{1,29},{... | collective-permute-start | bytes 393224 | tf_op jit(solution)/shard_map/ppermute | solution.py:32
  39.3 0.0 collective-permute-start.21
  39.3 9.6 %collective-permute-done.17.refs_1_ = bf16[256,256]{1,0:T(8,128)(2,1)S(1)} collective-permute-done((bf16[256,256]{1,0:T(8,128)(2,1)}, bf16[256,256]{1,0:T(8,128)(2,1)S(1)}, u32[]{:S(2)}, u32[]{:S(2)}) %collective-permute-start.17) | collective-permute-done | bytes 131104 | tf_op jit(solution)/shard_map/ppermute | solution.py:32
  48.9 2.0 %collective-permute-done.18.refs_2_ = bf16[256,256]{1,0:T(8,128)(2,1)S(1)} collective-permute-done((bf16[256,256]{1,0:T(8,128)(2,1)}, bf16[256,256]{1,0:T(8,128)(2,1)S(1)}, u32[]{:S(2)}, u32[]{:S(2)}) %collective-permute-start.18) | collective-permute-done | bytes 131104 | tf_op jit(solution)/shard_map/ppermute | solution.py:32
  50.9 0.5 collective-permute-start.23
  51.4 0.7 pad_maximum_fusion.weight
  52.2 4.4 %shard_map.52 = (bf16[112,256]{1,0:T(8,128)(2,1)}, bf16[112,256]{1,0:T(8,128)(2,1)}, bf16[112,256]{1,0:T(8,128)(2,1)}, bf16[112,256]{1,0:T(8,128)(2,1)}, bf16[11...) custom-call(f32[4,16,1024]{2,1,0:T(8,128)} %pad_maximum_fusion.weight, ...), custom_call_target="tpu_custom_call" | custom-call | tf_op jit(solution)/shard_map/pallas_call | solution.py:236
  56.6 0.0 collective-permute-done.19.refs_3_
  56.6 0.0 copy-start.21
  56.6 0.7 collective-permute-start.10
  57.2 0.0 collective-permute-done.20.refs_4_
  57.2 1.7 %collective-permute-start.11 = (bf16[112,256]{1,0:T(8,128)(2,1)}, bf16[112,256]{1,0:T(8,128)(2,1)S(1)}, u32[]{:S(2)}, u32[]{:S(2)}) collective-permute-start(bf16[112,256]{1,0:T(8,128)(2,1)} %get-tuple-element.48), channel_id=1, source_target_pairs={{0,20},{4,16},{8,28},{12,24},{16,4},{20,0},{24,12},{28,8},{1,21},{... | collective-permute-start | bytes 172040 | tf_op jit(solution)/shard_map/ppermute | solution.py:32
  59.0 2.9 %collective-permute-start.12 = (bf16[112,256]{1,0:T(8,128)(2,1)}, bf16[112,256]{1,0:T(8,128)(2,1)S(1)}, u32[]{:S(2)}, u32[]{:S(2)}) collective-permute-start(bf16[112,256]{1,0:T(8,128)(2,1)} %get-tuple-element.49), channel_id=1, source_target_pairs={{0,24},{4,28},{8,16},{12,20},{16,8},{20,12},{24,0},{28,4},{1,25},{... | collective-permute-start | bytes 172040 | tf_op jit(solution)/shard_map/ppermute | solution.py:32
  61.8 0.0 collective-permute-done.22.refs_6_
  61.8 1.0 %collective-permute-start.13 = (bf16[112,256]{1,0:T(8,128)(2,1)}, bf16[112,256]{1,0:T(8,128)(2,1)S(1)}, u32[]{:S(2)}, u32[]{:S(2)}) collective-permute-start(bf16[112,256]{1,0:T(8,128)(2,1)} %get-tuple-element.50), channel_id=1, source_target_pairs={{0,28},{4,24},{8,20},{12,16},{16,12},{20,8},{24,4},{28,0},{1,29},{... | collective-permute-start | bytes 172040 | tf_op jit(solution)/shard_map/ppermute | solution.py:32
  62.9 0.0 collective-permute-start.14
  62.9 0.6 copy-done.27
  63.5 4.4 %shard_map.54 = (bf16[112,256]{1,0:T(8,128)(2,1)}, bf16[112,256]{1,0:T(8,128)(2,1)}, bf16[112,256]{1,0:T(8,128)(2,1)}, bf16[112,256]{1,0:T(8,128)(2,1)}, bf16[11...) custom-call(f32[4,16,1024]{2,1,0:T(8,128)} %pad_maximum_fusion.weight, ...), custom_call_target="tpu_custom_call" | custom-call | tf_op jit(solution)/shard_map/pallas_call | solution.py:236
  67.9 0.9 collective-permute-start.15
  68.8 0.8 collective-permute-start.16
  69.6 1.6 %collective-permute-start.24 = (bf16[112,256]{1,0:T(8,128)(2,1)}, bf16[112,256]{1,0:T(8,128)(2,1)S(1)}, u32[]{:S(2)}, u32[]{:S(2)}) collective-permute-start(bf16[112,256]{1,0:T(8,128)(2,1)} %get-tuple-element.63), channel_id=1, source_target_pairs={{0,16},{4,20},{8,24},{12,28},{16,0},{20,4},{24,8},{28,12},{1,17},{... | collective-permute-start | bytes 172040 | tf_op jit(solution)/shard_map/ppermute | solution.py:32
  71.3 0.0 collective-permute-done.13.refs_4_
  71.3 0.7 collective-permute-start.25
  72.0 2.5 %collective-permute-start.26 = (bf16[112,256]{1,0:T(8,128)(2,1)}, bf16[112,256]{1,0:T(8,128)(2,1)S(1)}, u32[]{:S(2)}, u32[]{:S(2)}) collective-permute-start(bf16[112,256]{1,0:T(8,128)(2,1)} %get-tuple-element.65), channel_id=1, source_target_pairs={{0,24},{4,28},{8,16},{12,20},{16,8},{20,12},{24,0},{28,4},{1,25},{... | collective-permute-start | bytes 172040 | tf_op jit(solution)/shard_map/ppermute | solution.py:32
  74.5 1.3 %collective-permute-start.27 = (bf16[112,256]{1,0:T(8,128)(2,1)}, bf16[112,256]{1,0:T(8,128)(2,1)S(1)}, u32[]{:S(2)}, u32[]{:S(2)}) collective-permute-start(bf16[112,256]{1,0:T(8,128)(2,1)} %get-tuple-element.66), channel_id=1, source_target_pairs={{0,28},{4,24},{8,20},{12,16},{16,12},{20,8},{24,4},{28,0},{1,29},{... | collective-permute-start | bytes 172040 | tf_op jit(solution)/shard_map/ppermute | solution.py:32
  75.8 2.9 %collective-permute-done.24.refs_9_ = bf16[112,256]{1,0:T(8,128)(2,1)S(1)} collective-permute-done((bf16[112,256]{1,0:T(8,128)(2,1)}, bf16[112,256]{1,0:T(8,128)(2,1)S(1)}, u32[]{:S(2)}, u32[]{:S(2)}) %collective-permute-start.24) | collective-permute-done | bytes 57376 | tf_op jit(solution)/shard_map/ppermute | solution.py:32
  78.8 0.3 collective-permute-done.25.refs_10_
  79.1 1.9 %collective-permute-start.30 = (bf16[112,256]{1,0:T(8,128)(2,1)}, bf16[112,256]{1,0:T(8,128)(2,1)S(1)}, u32[]{:S(2)}, u32[]{:S(2)}) collective-permute-start(bf16[112,256]{1,0:T(8,128)(2,1)} %get-tuple-element.69), channel_id=1, source_target_pairs={{0,4},{4,0},{8,12},{12,8},{16,20},{20,16},{24,28},{28,24},{1,5},{5... | collective-permute-start | bytes 172040 | tf_op jit(solution)/shard_map/ppermute | solution.py:32
  81.0 0.0 collective-permute-done.26.refs_11_
  81.0 0.0 collective-permute-done.27.refs_12_
  81.1 1.0 %collective-permute-done.28.refs_13_ = bf16[112,256]{1,0:T(8,128)(2,1)S(1)} collective-permute-done((bf16[112,256]{1,0:T(8,128)(2,1)}, bf16[112,256]{1,0:T(8,128)(2,1)S(1)}, u32[]{:S(2)}, u32[]{:S(2)}) %collective-permute-start.28) | collective-permute-done | bytes 57376 | tf_op jit(solution)/shard_map/ppermute | solution.py:32
  82.1 1.2 %collective-permute-done.29.refs_14_ = bf16[112,256]{1,0:T(8,128)(2,1)S(1)} collective-permute-done((bf16[112,256]{1,0:T(8,128)(2,1)}, bf16[112,256]{1,0:T(8,128)(2,1)S(1)}, u32[]{:S(2)}, u32[]{:S(2)}) %collective-permute-start.29) | collective-permute-done | bytes 57376 | tf_op jit(solution)/shard_map/ppermute | solution.py:32
  83.3 0.5 copy-done.13
  83.8 0.0 copy-done.14
  83.9 1.6 %shard_map.56 = (f32[4,4,1024]{2,1,0:T(4,128)}, f32[4,4,1024]{2,1,0:T(4,128)}, f32[4,4,1024]{2,1,0:T(4,128)}, f32[4,4,1024]{2,1,0:T(4,128)}) custom-call(bf16[112,256]{1,0:T(8,128)(2,1)} %get-tuple-element.46.refs_0_, bf16[112,256]{1,0:T(8,128)(2,1)} %copy-done.1, bf16[112,256]{1,0:T(8,128)(2,1)} %copy-done.2, bf16[112,256]{1,0:T(8,128)(2,1)} %copy-done.3, ...), custom_call_target="tpu_custom_call" | custom-call | tf_op jit(solution)/shard_map/pallas_call | solution.py:254
  85.5 1.5 %collective-permute-start.33 = (f32[4,4,1024]{2,1,0:T(4,128)}, f32[4,4,1024]{2,1,0:T(4,128)S(1)}, u32[]{:S(2)}, u32[]{:S(2)}) collective-permute-start(f32[4,4,1024]{2,1,0:T(4,128)} %get-tuple-element.73), channel_id=1, source_target_pairs={{0,3},{1,2},{2,1},{3,0},{4,7},{5,6},{6,5},{7,4},{8,11},{9,10},{10,... | collective-permute-start | bytes 196616 | tf_op jit(solution)/shard_map/ppermute | solution.py:32
  87.0 0.5 collective-permute-start.32
  87.5 1.5 %collective-permute-start.31 = (f32[4,4,1024]{2,1,0:T(4,128)}, f32[4,4,1024]{2,1,0:T(4,128)S(1)}, u32[]{:S(2)}, u32[]{:S(2)}) collective-permute-start(f32[4,4,1024]{2,1,0:T(4,128)} %get-tuple-element.71), channel_id=1, source_target_pairs={{0,1},{1,0},{2,3},{3,2},{4,5},{5,4},{6,7},{7,6},{8,9},{9,8},{10,11... | collective-permute-start | bytes 196616 | tf_op jit(solution)/shard_map/ppermute | solution.py:32
  89.0 3.0 %shard_map.55 = bf16[128,4096]{1,0:T(8,128)(2,1)} custom-call(f32[4,16,1024]{2,1,0:T(8,128)} %pad_maximum_fusion.weight, bf16[112,256]{1,0:T(8,128)(2,1)} %get-tuple-element.46.refs_0_, bf16[112,256]{1,0:T(8,128)(2,1)} %copy-done.1, bf16[112,256]{1,0:T(8,128)(2,1)} %copy-done.2, bf16[112,256]{1,0:T(8,128)(2,1)} %copy-done.3, bf16[112,256]{1,0:T(8,128)(2,1)} %copy-done.4, ...), custom_call_target="tpu_custom_call" | custom-call | tf_op jit(solution)/shard_map/pallas_call | solution.py:265
  92.0 0.1 collective-permute-done.32
  92.1 0.1 collective-permute-done.31
  92.2 0.6 add_add_fusion
  (87 shorter events, 0.2 us)
Async XLA Ops:
  1.5 11.6 %collective-permute-start.2 = (f32[16,1024]{1,0:T(8,128)S(1)}, f32[16,1024]{1,0:T(8,128)S(1)}, u32[]{:S(2)}, u32[]{:S(2)}) collective-permute-start(f32[16,1024]{1,0:T(8,128)S(1)} %reshape.7), channel_id=1, source_target_pairs={{0,3},{1,2},{2,1},{3,0},{4,7},{5,6},{6,5},{7,4},{8,11},{9,10},{10,... | collective-permute-start | bytes 196616 | tf_op jit(solution)/shard_map/ppermute | solution.py:32
  5.5 8.8 %collective-permute-start.1 = (f32[16,1024]{1,0:T(8,128)S(1)}, f32[16,1024]{1,0:T(8,128)S(1)}, u32[]{:S(2)}, u32[]{:S(2)}) collective-permute-start(f32[16,1024]{1,0:T(8,128)S(1)} %reshape.7), channel_id=1, source_target_pairs={{0,2},{1,3},{2,0},{3,1},{4,6},{5,7},{6,4},{7,5},{8,10},{9,11},{10,... | collective-permute-start | bytes 196616 | tf_op jit(solution)/shard_map/ppermute | solution.py:32
  7.9 18.3 %collective-permute-start.3 = (bf16[256,256]{1,0:T(8,128)(2,1)}, bf16[256,256]{1,0:T(8,128)(2,1)S(1)}, u32[]{:S(2)}, u32[]{:S(2)}) collective-permute-start(bf16[256,256]{1,0:T(8,128)(2,1)} %get-tuple-element.39), channel_id=1, source_target_pairs={{0,16},{4,20},{8,24},{12,28},{16,0},{20,4},{24,8},{28,12},{1,17},{... | collective-permute-start | bytes 393224 | tf_op jit(solution)/shard_map/ppermute | solution.py:32
  10.6 16.2 %collective-permute-start.4 = (bf16[256,256]{1,0:T(8,128)(2,1)}, bf16[256,256]{1,0:T(8,128)(2,1)S(1)}, u32[]{:S(2)}, u32[]{:S(2)}) collective-permute-start(bf16[256,256]{1,0:T(8,128)(2,1)} %get-tuple-element.40), channel_id=1, source_target_pairs={{0,20},{4,16},{8,28},{12,24},{16,4},{20,0},{24,12},{28,8},{1,21},{... | collective-permute-start | bytes 393224 | tf_op jit(solution)/shard_map/ppermute | solution.py:32
  10.6 18.2 %collective-permute-start.5 = (bf16[256,256]{1,0:T(8,128)(2,1)}, bf16[256,256]{1,0:T(8,128)(2,1)S(1)}, u32[]{:S(2)}, u32[]{:S(2)}) collective-permute-start(bf16[256,256]{1,0:T(8,128)(2,1)} %get-tuple-element.41), channel_id=1, source_target_pairs={{0,24},{4,28},{8,16},{12,20},{16,8},{20,12},{24,0},{28,4},{1,25},{... | collective-permute-start | bytes 393224 | tf_op jit(solution)/shard_map/ppermute | solution.py:32
  13.1 20.2 %collective-permute-start.6 = (bf16[256,256]{1,0:T(8,128)(2,1)}, bf16[256,256]{1,0:T(8,128)(2,1)S(1)}, u32[]{:S(2)}, u32[]{:S(2)}) collective-permute-start(bf16[256,256]{1,0:T(8,128)(2,1)} %get-tuple-element.42), channel_id=1, source_target_pairs={{0,28},{4,24},{8,20},{12,16},{16,12},{20,8},{24,4},{28,0},{1,29},{... | collective-permute-start | bytes 393224 | tf_op jit(solution)/shard_map/ppermute | solution.py:32
  14.3 5.0 %collective-permute-start = (f32[16,1024]{1,0:T(8,128)S(1)}, f32[16,1024]{1,0:T(8,128)S(1)}, u32[]{:S(2)}, u32[]{:S(2)}) collective-permute-start(f32[16,1024]{1,0:T(8,128)S(1)} %reshape.7), channel_id=1, source_target_pairs={{0,1},{1,0},{2,3},{3,2},{4,5},{5,4},{6,7},{7,6},{8,9},{9,8},{10,11... | collective-permute-start | bytes 196616 | tf_op jit(solution)/shard_map/ppermute | solution.py:32
  16.7 2.5 %copy-start.33 = (bf16[256,256]{1,0:T(8,128)(2,1)S(1)}, bf16[256,256]{1,0:T(8,128)(2,1)}, u32[]{:S(2)}) copy-start(bf16[256,256]{1,0:T(8,128)(2,1)} %get-tuple-element.43) | copy-start | bytes 393220
  16.7 9.5 %copy-start.32 = (bf16[256,256]{1,0:T(8,128)(2,1)S(1)}, bf16[256,256]{1,0:T(8,128)(2,1)}, u32[]{:S(2)}) copy-start(bf16[256,256]{1,0:T(8,128)(2,1)} %get-tuple-element.44) | copy-start | bytes 393220
  16.7 10.1 %copy-start.31 = (bf16[256,256]{1,0:T(8,128)(2,1)S(1)}, bf16[256,256]{1,0:T(8,128)(2,1)}, u32[]{:S(2)}) copy-start(bf16[256,256]{1,0:T(8,128)(2,1)} %get-tuple-element.45) | copy-start | bytes 393220
  16.7 32.1 %copy-start = (f32[4,4,1024]{2,1,0:T(4,128)S(1)}, f32[4,4,1024]{2,1,0:T(4,128)}, u32[]{:S(2)}) copy-start(f32[4,4,1024]{2,1,0:T(4,128)} %param.5) | copy-start | bytes 196612
  19.2 31.7 %copy-start.30 = (bf16[256,256]{1,0:T(8,128)(2,1)S(1)}, bf16[256,256]{1,0:T(8,128)(2,1)}, u32[]{:S(2)}) copy-start(bf16[256,256]{1,0:T(8,128)(2,1)} %get-tuple-element.61) | copy-start | bytes 393220
  19.3 16.4 %collective-permute-start.7 = (bf16[256,256]{1,0:T(8,128)(2,1)S(1)}, bf16[256,256]{1,0:T(8,128)(2,1)S(1)}, u32[]{:S(2)}, u32[]{:S(2)}) collective-permute-start(bf16[256,256]{1,0:T(8,128)(2,1)S(1)} %copy-done.33), channel_id=1, source_target_pairs={{0,8},{4,12},{8,0},{12,4},{16,24},{20,28},{24,16},{28,20},{1,9},{5... | collective-permute-start | bytes 393224 | tf_op jit(solution)/shard_map/ppermute | solution.py:32
  26.2 25.9 %copy-start.15 = (bf16[256,256]{1,0:T(8,128)(2,1)}, bf16[256,256]{1,0:T(8,128)(2,1)S(1)}, u32[]{:S(2)}) copy-start(bf16[256,256]{1,0:T(8,128)(2,1)S(1)} %collective-permute-done.3.refs_1_) | copy-start | bytes 393220
  26.2 10.0 %collective-permute-start.8 = (bf16[256,256]{1,0:T(8,128)(2,1)S(1)}, bf16[256,256]{1,0:T(8,128)(2,1)S(1)}, u32[]{:S(2)}, u32[]{:S(2)}) collective-permute-start(bf16[256,256]{1,0:T(8,128)(2,1)S(1)} %copy-done.32), channel_id=1, source_target_pairs={{0,12},{4,8},{8,4},{12,0},{16,28},{20,24},{24,20},{28,16},{1,13},{... | collective-permute-start | bytes 393224 | tf_op jit(solution)/shard_map/ppermute | solution.py:32
  26.8 25.4 %copy-start.16 = (bf16[256,256]{1,0:T(8,128)(2,1)}, bf16[256,256]{1,0:T(8,128)(2,1)S(1)}, u32[]{:S(2)}) copy-start(bf16[256,256]{1,0:T(8,128)(2,1)S(1)} %collective-permute-done.4.refs_2_) | copy-start | bytes 393220
  26.8 12.4 %collective-permute-start.9 = (bf16[256,256]{1,0:T(8,128)(2,1)S(1)}, bf16[256,256]{1,0:T(8,128)(2,1)S(1)}, u32[]{:S(2)}, u32[]{:S(2)}) collective-permute-start(bf16[256,256]{1,0:T(8,128)(2,1)S(1)} %copy-done.31), channel_id=1, source_target_pairs={{0,4},{4,0},{8,12},{12,8},{16,20},{20,16},{24,28},{28,24},{1,5},{5... | collective-permute-start | bytes 393224 | tf_op jit(solution)/shard_map/ppermute | solution.py:32
  28.8 23.4 %copy-start.17 = (bf16[256,256]{1,0:T(8,128)(2,1)}, bf16[256,256]{1,0:T(8,128)(2,1)S(1)}, u32[]{:S(2)}) copy-start(bf16[256,256]{1,0:T(8,128)(2,1)S(1)} %collective-permute-done.5.refs_3_) | copy-start | bytes 393220
  28.8 20.0 %collective-permute-start.17 = (bf16[256,256]{1,0:T(8,128)(2,1)}, bf16[256,256]{1,0:T(8,128)(2,1)S(1)}, u32[]{:S(2)}, u32[]{:S(2)}) collective-permute-start(bf16[256,256]{1,0:T(8,128)(2,1)} %get-tuple-element.55), channel_id=1, source_target_pairs={{0,16},{4,20},{8,24},{12,28},{16,0},{20,4},{24,8},{28,12},{1,17},{... | collective-permute-start | bytes 393224 | tf_op jit(solution)/shard_map/ppermute | solution.py:32
  33.4 18.8 %copy-start.19 = (bf16[256,256]{1,0:T(8,128)(2,1)}, bf16[256,256]{1,0:T(8,128)(2,1)S(1)}, u32[]{:S(2)}) copy-start(bf16[256,256]{1,0:T(8,128)(2,1)S(1)} %collective-permute-done.6.refs_4_) | copy-start | bytes 393220
  33.4 17.6 %collective-permute-start.18 = (bf16[256,256]{1,0:T(8,128)(2,1)}, bf16[256,256]{1,0:T(8,128)(2,1)S(1)}, u32[]{:S(2)}, u32[]{:S(2)}) collective-permute-start(bf16[256,256]{1,0:T(8,128)(2,1)} %get-tuple-element.56), channel_id=1, source_target_pairs={{0,20},{4,16},{8,28},{12,24},{16,4},{20,0},{24,12},{28,8},{1,21},{... | collective-permute-start | bytes 393224 | tf_op jit(solution)/shard_map/ppermute | solution.py:32
  35.7 16.5 %copy-start.24 = (bf16[256,256]{1,0:T(8,128)(2,1)}, bf16[256,256]{1,0:T(8,128)(2,1)S(1)}, u32[]{:S(2)}) copy-start(bf16[256,256]{1,0:T(8,128)(2,1)S(1)} %collective-permute-done.7.refs_5_) | copy-start | bytes 393220
  35.7 20.9 %collective-permute-start.19 = (bf16[256,256]{1,0:T(8,128)(2,1)}, bf16[256,256]{1,0:T(8,128)(2,1)S(1)}, u32[]{:S(2)}, u32[]{:S(2)}) collective-permute-start(bf16[256,256]{1,0:T(8,128)(2,1)} %get-tuple-element.57), channel_id=1, source_target_pairs={{0,24},{4,28},{8,16},{12,20},{16,8},{20,12},{24,0},{28,4},{1,25},{... | collective-permute-start | bytes 393224 | tf_op jit(solution)/shard_map/ppermute | solution.py:32
  36.3 15.9 %copy-start.26 = (bf16[256,256]{1,0:T(8,128)(2,1)}, bf16[256,256]{1,0:T(8,128)(2,1)S(1)}, u32[]{:S(2)}) copy-start(bf16[256,256]{1,0:T(8,128)(2,1)S(1)} %collective-permute-done.8.refs_6_) | copy-start | bytes 393220
  36.3 21.0 %collective-permute-start.20 = (bf16[256,256]{1,0:T(8,128)(2,1)}, bf16[256,256]{1,0:T(8,128)(2,1)S(1)}, u32[]{:S(2)}, u32[]{:S(2)}) collective-permute-start(bf16[256,256]{1,0:T(8,128)(2,1)} %get-tuple-element.58), channel_id=1, source_target_pairs={{0,28},{4,24},{8,20},{12,16},{16,12},{20,8},{24,4},{28,0},{1,29},{... | collective-permute-start | bytes 393224 | tf_op jit(solution)/shard_map/ppermute | solution.py:32
  39.3 12.9 %copy-start.28 = (bf16[256,256]{1,0:T(8,128)(2,1)}, bf16[256,256]{1,0:T(8,128)(2,1)S(1)}, u32[]{:S(2)}) copy-start(bf16[256,256]{1,0:T(8,128)(2,1)S(1)} %collective-permute-done.9.refs_7_) | copy-start | bytes 393220
  39.3 19.7 %collective-permute-start.21 = (bf16[256,256]{1,0:T(8,128)(2,1)}, bf16[256,256]{1,0:T(8,128)(2,1)S(1)}, u32[]{:S(2)}, u32[]{:S(2)}) collective-permute-start(bf16[256,256]{1,0:T(8,128)(2,1)} %get-tuple-element.59), channel_id=1, source_target_pairs={{0,8},{4,12},{8,0},{12,4},{16,24},{20,28},{24,16},{28,20},{1,9},{5... | collective-permute-start | bytes 393224 | tf_op jit(solution)/shard_map/ppermute | solution.py:32
  48.9 3.3 %copy-start.18 = (bf16[256,256]{1,0:T(8,128)(2,1)}, bf16[256,256]{1,0:T(8,128)(2,1)S(1)}, u32[]{:S(2)}) copy-start(bf16[256,256]{1,0:T(8,128)(2,1)S(1)} %collective-permute-done.17.refs_1_) | copy-start | bytes 393220
  48.9 13.0 %collective-permute-start.22 = (bf16[256,256]{1,0:T(8,128)(2,1)}, bf16[256,256]{1,0:T(8,128)(2,1)S(1)}, u32[]{:S(2)}, u32[]{:S(2)}) collective-permute-start(bf16[256,256]{1,0:T(8,128)(2,1)} %get-tuple-element.60), channel_id=1, source_target_pairs={{0,12},{4,8},{8,4},{12,0},{16,28},{20,24},{24,20},{28,16},{1,13},{... | collective-permute-start | bytes 393224 | tf_op jit(solution)/shard_map/ppermute | solution.py:32
  50.9 5.6 %copy-start.20 = (bf16[256,256]{1,0:T(8,128)(2,1)}, bf16[256,256]{1,0:T(8,128)(2,1)S(1)}, u32[]{:S(2)}) copy-start(bf16[256,256]{1,0:T(8,128)(2,1)S(1)} %collective-permute-done.18.refs_2_) | copy-start | bytes 393220
  50.9 11.9 %collective-permute-start.23 = (bf16[256,256]{1,0:T(8,128)(2,1)S(1)}, bf16[256,256]{1,0:T(8,128)(2,1)S(1)}, u32[]{:S(2)}, u32[]{:S(2)}) collective-permute-start(bf16[256,256]{1,0:T(8,128)(2,1)S(1)} %copy-done.30), channel_id=1, source_target_pairs={{0,4},{4,0},{8,12},{12,8},{16,20},{20,16},{24,28},{28,24},{1,5},{5... | collective-permute-start | bytes 393224 | tf_op jit(solution)/shard_map/ppermute | solution.py:32
  56.6 6.3 %copy-start.21 = (bf16[256,256]{1,0:T(8,128)(2,1)}, bf16[256,256]{1,0:T(8,128)(2,1)S(1)}, u32[]{:S(2)}) copy-start(bf16[256,256]{1,0:T(8,128)(2,1)S(1)} %collective-permute-done.19.refs_3_) | copy-start | bytes 393220
  56.6 11.3 %collective-permute-start.10 = (bf16[112,256]{1,0:T(8,128)(2,1)}, bf16[112,256]{1,0:T(8,128)(2,1)S(1)}, u32[]{:S(2)}, u32[]{:S(2)}) collective-permute-start(bf16[112,256]{1,0:T(8,128)(2,1)} %get-tuple-element.47), channel_id=1, source_target_pairs={{0,16},{4,20},{8,24},{12,28},{16,0},{20,4},{24,8},{28,12},{1,17},{... | collective-permute-start | bytes 172040 | tf_op jit(solution)/shard_map/ppermute | solution.py:32
  57.2 5.6 %copy-start.22 = (bf16[256,256]{1,0:T(8,128)(2,1)}, bf16[256,256]{1,0:T(8,128)(2,1)S(1)}, u32[]{:S(2)}) copy-start(bf16[256,256]{1,0:T(8,128)(2,1)S(1)} %collective-permute-done.20.refs_4_) | copy-start | bytes 393220
  57.2 11.6 %collective-permute-start.11 = (bf16[112,256]{1,0:T(8,128)(2,1)}, bf16[112,256]{1,0:T(8,128)(2,1)S(1)}, u32[]{:S(2)}, u32[]{:S(2)}) collective-permute-start(bf16[112,256]{1,0:T(8,128)(2,1)} %get-tuple-element.48), channel_id=1, source_target_pairs={{0,20},{4,16},{8,28},{12,24},{16,4},{20,0},{24,12},{28,8},{1,21},{... | collective-permute-start | bytes 172040 | tf_op jit(solution)/shard_map/ppermute | solution.py:32
  58.9 3.9 %copy-start.23 = (bf16[256,256]{1,0:T(8,128)(2,1)}, bf16[256,256]{1,0:T(8,128)(2,1)S(1)}, u32[]{:S(2)}) copy-start(bf16[256,256]{1,0:T(8,128)(2,1)S(1)} %collective-permute-done.21.refs_5_) | copy-start | bytes 393220
  59.0 10.7 %collective-permute-start.12 = (bf16[112,256]{1,0:T(8,128)(2,1)}, bf16[112,256]{1,0:T(8,128)(2,1)S(1)}, u32[]{:S(2)}, u32[]{:S(2)}) collective-permute-start(bf16[112,256]{1,0:T(8,128)(2,1)} %get-tuple-element.49), channel_id=1, source_target_pairs={{0,24},{4,28},{8,16},{12,20},{16,8},{20,12},{24,0},{28,4},{1,25},{... | collective-permute-start | bytes 172040 | tf_op jit(solution)/shard_map/ppermute | solution.py:32
  61.8 9.4 %collective-permute-start.13 = (bf16[112,256]{1,0:T(8,128)(2,1)}, bf16[112,256]{1,0:T(8,128)(2,1)S(1)}, u32[]{:S(2)}, u32[]{:S(2)}) collective-permute-start(bf16[112,256]{1,0:T(8,128)(2,1)} %get-tuple-element.50), channel_id=1, source_target_pairs={{0,28},{4,24},{8,20},{12,16},{16,12},{20,8},{24,4},{28,0},{1,29},{... | collective-permute-start | bytes 172040 | tf_op jit(solution)/shard_map/ppermute | solution.py:32
  62.9 9.1 %collective-permute-start.14 = (bf16[112,256]{1,0:T(8,128)(2,1)}, bf16[112,256]{1,0:T(8,128)(2,1)S(1)}, u32[]{:S(2)}, u32[]{:S(2)}) collective-permute-start(bf16[112,256]{1,0:T(8,128)(2,1)} %get-tuple-element.51), channel_id=1, source_target_pairs={{0,8},{4,12},{8,0},{12,4},{16,24},{20,28},{24,16},{28,20},{1,9},{5... | collective-permute-start | bytes 172040 | tf_op jit(solution)/shard_map/ppermute | solution.py:32
  63.5 4.4 %copy-start.35 = (bf16[112,256]{1,0:T(8,128)(2,1)S(1)}, bf16[112,256]{1,0:T(8,128)(2,1)}, u32[]{:S(2)}) copy-start(bf16[112,256]{1,0:T(8,128)(2,1)} %get-tuple-element.52) | copy-start | bytes 172036
  63.5 5.3 %copy-start.34 = (bf16[112,256]{1,0:T(8,128)(2,1)S(1)}, bf16[112,256]{1,0:T(8,128)(2,1)}, u32[]{:S(2)}) copy-start(bf16[112,256]{1,0:T(8,128)(2,1)} %get-tuple-element.53) | copy-start | bytes 172036
  67.9 15.3 %copy-start.1 = (bf16[112,256]{1,0:T(8,128)(2,1)}, bf16[112,256]{1,0:T(8,128)(2,1)S(1)}, u32[]{:S(2)}) copy-start(bf16[112,256]{1,0:T(8,128)(2,1)S(1)} %collective-permute-done.10.refs_1_) | copy-start | bytes 172036
  67.9 6.6 %collective-permute-start.15 = (bf16[112,256]{1,0:T(8,128)(2,1)S(1)}, bf16[112,256]{1,0:T(8,128)(2,1)S(1)}, u32[]{:S(2)}, u32[]{:S(2)}) collective-permute-start(bf16[112,256]{1,0:T(8,128)(2,1)S(1)} %copy-done.35), channel_id=1, source_target_pairs={{0,12},{4,8},{8,4},{12,0},{16,28},{20,24},{24,20},{28,16},{1,13},{... | collective-permute-start | bytes 172040 | tf_op jit(solution)/shard_map/ppermute | solution.py:32
  68.8 14.4 %copy-start.2 = (bf16[112,256]{1,0:T(8,128)(2,1)}, bf16[112,256]{1,0:T(8,128)(2,1)S(1)}, u32[]{:S(2)}) copy-start(bf16[112,256]{1,0:T(8,128)(2,1)S(1)} %collective-permute-done.11.refs_2_) | copy-start | bytes 172036
  68.8 7.0 %collective-permute-start.16 = (bf16[112,256]{1,0:T(8,128)(2,1)S(1)}, bf16[112,256]{1,0:T(8,128)(2,1)S(1)}, u32[]{:S(2)}, u32[]{:S(2)}) collective-permute-start(bf16[112,256]{1,0:T(8,128)(2,1)S(1)} %copy-done.34), channel_id=1, source_target_pairs={{0,4},{4,0},{8,12},{12,8},{16,20},{20,16},{24,28},{28,24},{1,5},{5... | collective-permute-start | bytes 172040 | tf_op jit(solution)/shard_map/ppermute | solution.py:32
  69.6 13.6 %copy-start.3 = (bf16[112,256]{1,0:T(8,128)(2,1)}, bf16[112,256]{1,0:T(8,128)(2,1)S(1)}, u32[]{:S(2)}) copy-start(bf16[112,256]{1,0:T(8,128)(2,1)S(1)} %collective-permute-done.12.refs_3_) | copy-start | bytes 172036
  69.6 9.2 %collective-permute-start.24 = (bf16[112,256]{1,0:T(8,128)(2,1)}, bf16[112,256]{1,0:T(8,128)(2,1)S(1)}, u32[]{:S(2)}, u32[]{:S(2)}) collective-permute-start(bf16[112,256]{1,0:T(8,128)(2,1)} %get-tuple-element.63), channel_id=1, source_target_pairs={{0,16},{4,20},{8,24},{12,28},{16,0},{20,4},{24,8},{28,12},{1,17},{... | collective-permute-start | bytes 172040 | tf_op jit(solution)/shard_map/ppermute | solution.py:32
  71.3 12.0 %copy-start.4 = (bf16[112,256]{1,0:T(8,128)(2,1)}, bf16[112,256]{1,0:T(8,128)(2,1)S(1)}, u32[]{:S(2)}) copy-start(bf16[112,256]{1,0:T(8,128)(2,1)S(1)} %collective-permute-done.13.refs_4_) | copy-start | bytes 172036
  71.3 7.9 %collective-permute-start.25 = (bf16[112,256]{1,0:T(8,128)(2,1)}, bf16[112,256]{1,0:T(8,128)(2,1)S(1)}, u32[]{:S(2)}, u32[]{:S(2)}) collective-permute-start(bf16[112,256]{1,0:T(8,128)(2,1)} %get-tuple-element.64), channel_id=1, source_target_pairs={{0,20},{4,16},{8,28},{12,24},{16,4},{20,0},{24,12},{28,8},{1,21},{... | collective-permute-start | bytes 172040 | tf_op jit(solution)/shard_map/ppermute | solution.py:32
  72.0 11.3 %copy-start.5 = (bf16[112,256]{1,0:T(8,128)(2,1)}, bf16[112,256]{1,0:T(8,128)(2,1)S(1)}, u32[]{:S(2)}) copy-start(bf16[112,256]{1,0:T(8,128)(2,1)S(1)} %collective-permute-done.14.refs_5_) | copy-start | bytes 172036
  72.0 9.1 %collective-permute-start.26 = (bf16[112,256]{1,0:T(8,128)(2,1)}, bf16[112,256]{1,0:T(8,128)(2,1)S(1)}, u32[]{:S(2)}, u32[]{:S(2)}) collective-permute-start(bf16[112,256]{1,0:T(8,128)(2,1)} %get-tuple-element.65), channel_id=1, source_target_pairs={{0,24},{4,28},{8,16},{12,20},{16,8},{20,12},{24,0},{28,4},{1,25},{... | collective-permute-start | bytes 172040 | tf_op jit(solution)/shard_map/ppermute | solution.py:32
  74.5 8.7 %copy-start.6 = (bf16[112,256]{1,0:T(8,128)(2,1)}, bf16[112,256]{1,0:T(8,128)(2,1)S(1)}, u32[]{:S(2)}) copy-start(bf16[112,256]{1,0:T(8,128)(2,1)S(1)} %collective-permute-done.15.refs_6_) | copy-start | bytes 172036
  74.5 6.5 %collective-permute-start.27 = (bf16[112,256]{1,0:T(8,128)(2,1)}, bf16[112,256]{1,0:T(8,128)(2,1)S(1)}, u32[]{:S(2)}, u32[]{:S(2)}) collective-permute-start(bf16[112,256]{1,0:T(8,128)(2,1)} %get-tuple-element.66), channel_id=1, source_target_pairs={{0,28},{4,24},{8,20},{12,16},{16,12},{20,8},{24,4},{28,0},{1,29},{... | collective-permute-start | bytes 172040 | tf_op jit(solution)/shard_map/ppermute | solution.py:32
  75.8 7.4 %copy-start.7 = (bf16[112,256]{1,0:T(8,128)(2,1)}, bf16[112,256]{1,0:T(8,128)(2,1)S(1)}, u32[]{:S(2)}) copy-start(bf16[112,256]{1,0:T(8,128)(2,1)S(1)} %collective-permute-done.16.refs_7_) | copy-start | bytes 172036
  75.8 6.2 %collective-permute-start.28 = (bf16[112,256]{1,0:T(8,128)(2,1)}, bf16[112,256]{1,0:T(8,128)(2,1)S(1)}, u32[]{:S(2)}, u32[]{:S(2)}) collective-permute-start(bf16[112,256]{1,0:T(8,128)(2,1)} %get-tuple-element.67), channel_id=1, source_target_pairs={{0,8},{4,12},{8,0},{12,4},{16,24},{20,28},{24,16},{28,20},{1,9},{5... | collective-permute-start | bytes 172040 | tf_op jit(solution)/shard_map/ppermute | solution.py:32
  78.8 4.5 %copy-start.8 = (bf16[112,256]{1,0:T(8,128)(2,1)}, bf16[112,256]{1,0:T(8,128)(2,1)S(1)}, u32[]{:S(2)}) copy-start(bf16[112,256]{1,0:T(8,128)(2,1)S(1)} %collective-permute-done.24.refs_9_) | copy-start | bytes 172036
  78.8 4.4 %collective-permute-start.29 = (bf16[112,256]{1,0:T(8,128)(2,1)}, bf16[112,256]{1,0:T(8,128)(2,1)S(1)}, u32[]{:S(2)}, u32[]{:S(2)}) collective-permute-start(bf16[112,256]{1,0:T(8,128)(2,1)} %get-tuple-element.68), channel_id=1, source_target_pairs={{0,12},{4,8},{8,4},{12,0},{16,28},{20,24},{24,20},{28,16},{1,13},{... | collective-permute-start | bytes 172040 | tf_op jit(solution)/shard_map/ppermute | solution.py:32
  79.1 4.2 %copy-start.9 = (bf16[112,256]{1,0:T(8,128)(2,1)}, bf16[112,256]{1,0:T(8,128)(2,1)S(1)}, u32[]{:S(2)}) copy-start(bf16[112,256]{1,0:T(8,128)(2,1)S(1)} %collective-permute-done.25.refs_10_) | copy-start | bytes 172036
  79.1 4.1 %collective-permute-start.30 = (bf16[112,256]{1,0:T(8,128)(2,1)}, bf16[112,256]{1,0:T(8,128)(2,1)S(1)}, u32[]{:S(2)}, u32[]{:S(2)}) collective-permute-start(bf16[112,256]{1,0:T(8,128)(2,1)} %get-tuple-element.69), channel_id=1, source_target_pairs={{0,4},{4,0},{8,12},{12,8},{16,20},{20,16},{24,28},{28,24},{1,5},{5... | collective-permute-start | bytes 172040 | tf_op jit(solution)/shard_map/ppermute | solution.py:32
  81.1 2.3 %copy-start.11 = (bf16[112,256]{1,0:T(8,128)(2,1)}, bf16[112,256]{1,0:T(8,128)(2,1)S(1)}, u32[]{:S(2)}) copy-start(bf16[112,256]{1,0:T(8,128)(2,1)S(1)} %collective-permute-done.27.refs_12_) | copy-start | bytes 172036
  85.5 6.6 %collective-permute-start.33 = (f32[4,4,1024]{2,1,0:T(4,128)}, f32[4,4,1024]{2,1,0:T(4,128)S(1)}, u32[]{:S(2)}, u32[]{:S(2)}) collective-permute-start(f32[4,4,1024]{2,1,0:T(4,128)} %get-tuple-element.73), channel_id=1, source_target_pairs={{0,3},{1,2},{2,1},{3,0},{4,7},{5,6},{6,5},{7,4},{8,11},{9,10},{10,... | collective-permute-start | bytes 196616 | tf_op jit(solution)/shard_map/ppermute | solution.py:32
  87.0 5.1 %collective-permute-start.32 = (f32[4,4,1024]{2,1,0:T(4,128)}, f32[4,4,1024]{2,1,0:T(4,128)S(1)}, u32[]{:S(2)}, u32[]{:S(2)}) collective-permute-start(f32[4,4,1024]{2,1,0:T(4,128)} %get-tuple-element.72), channel_id=1, source_target_pairs={{0,2},{1,3},{2,0},{3,1},{4,6},{5,7},{6,4},{7,5},{8,10},{9,11},{10,... | collective-permute-start | bytes 196616 | tf_op jit(solution)/shard_map/ppermute | solution.py:32
  87.5 4.7 %copy-start.29 = (f32[4,4,1024]{2,1,0:T(4,128)S(1)}, f32[4,4,1024]{2,1,0:T(4,128)}, u32[]{:S(2)}) copy-start(f32[4,4,1024]{2,1,0:T(4,128)} %get-tuple-element.70) | copy-start | bytes 196612
  87.5 4.7 %collective-permute-start.31 = (f32[4,4,1024]{2,1,0:T(4,128)}, f32[4,4,1024]{2,1,0:T(4,128)S(1)}, u32[]{:S(2)}, u32[]{:S(2)}) collective-permute-start(f32[4,4,1024]{2,1,0:T(4,128)} %get-tuple-element.71), channel_id=1, source_target_pairs={{0,1},{1,0},{2,3},{3,2},{4,5},{5,4},{6,7},{7,6},{8,9},{9,8},{10,11... | collective-permute-start | bytes 196616 | tf_op jit(solution)/shard_map/ppermute | solution.py:32
  (6 other events, 6.5 us)
where the time goes:
time: 93.3 us; the launch traced here: 92.9 us
  starting transfers between devices  43.9 us (47%)
  waiting for transfers between devices  24.8 us (27%)
  Pallas kernels  19.7 us (21%)
  local copies, waits for them, and re-layouts  2.16 us (2%)
  other arithmetic  1.37 us (1%)
  between operations  0.99 us (1%)
    ppermute x34, starting transfers between devices, send(): return lax.ppermute(block, axis, [(s, s ^ message) for s in range(n)])  43.9 us
    ppermute x34, waiting for transfers between devices, send(): return lax.ppermute(block, axis, [(s, s ^ message) for s in range(n)])  24.8 us
    pallas_call x2, Pallas kernels, per_device(): pl.pallas_call(functools.partial(block_kernel, n, nd, rc, wide, c * cw),...  8.75 us
    pallas_call x3, Pallas kernels, per_device(): pl.pallas_call(functools.partial(cut_kernel, n, wide, c * cw, which), out...  6.31 us
    pallas_call x1, Pallas kernels, per_device(): pl.pallas_call(functools.partial(spread_kernel, n, nd, wide), out_shape=s...  3.03 us
  transfers between devices with their start and end apart: 34, of which 10 were waited for; matrix products, arithmetic and copies ran while one was open for 1% of the time, Pallas kernels for 19%

commit v1 on v0

--- a/solution.py
+++ b/solution.py
@@ -170,29 +170,34 @@
         outs[k][...] = held[lax.bitwise_xor(col, jnp.int32(k))]
 
 
-def spread_kernel(n, nd, wide, weight, *refs):
-    blocks, out = refs[:-1], refs[-1]
+def spread_kernel(n, nd, wide, first, weight, *refs):
+    blocks, (out, made_ref, sem) = refs[:n], refs[-3:]
     place, col, share = places(n), lax.axis_index("dp"), n // nd
-    rc = out.shape[0] // POOL
-    cw = blocks[0].shape[1]
-    sel = interleave_matrix(rc * POOL)
-    for c in range(len(blocks) // n):
-        for i in range(n):
-            ref = blocks[c * n + i]
-            cols = pl.ds(pl.multiple_of(place[i] * wide + c * cw, HEAD_DIM), cw)
-            w = weight[
-                lax.bitwise_xor(col, lax.div(place[i], share)),
-                :,
-                pl.ds(pl.multiple_of(lax.rem(place[i], share) * wide + c * cw, HEAD_DIM), cw),
-            ]
-            parts = [ref[t * rc : (t + 1) * rc, :].astype(F32) for t in range(3)]
-            made = []
-            for j in range(POOL):
-                total = parts[0] * w[j][None, :]
-                for t in range(1, 3):
-                    total = total + parts[t] * w[t * POOL + j][None, :]
-                made.append(total.astype(BF16))
-            out[:, cols] = dot(sel, jnp.concatenate(made, 0), 0, 0).astype(BF16)
+    rows, cw = made_ref.shape[1:]
+    rc = rows // POOL
+    sel = interleave_matrix(rows)
+    copies = []
+    for i in range(n):
+        ref = blocks[i]
+        w = weight[
+            lax.bitwise_xor(col, lax.div(place[i], share)),
+            :,
+            pl.ds(pl.multiple_of(lax.rem(place[i], share) * wide + first, HEAD_DIM), cw),
+        ]
+        parts = [ref[t * rc : (t + 1) * rc, :].astype(F32) for t in range(3)]
+        made = []
+        for j in range(POOL):
+            total = parts[0] * w[j][None, :]
+            for t in range(1, 3):
+                total = total + parts[t] * w[t * POOL + j][None, :]
+            made.append(total.astype(BF16))
+        made_ref[i] = dot(sel, jnp.concatenate(made, 0), 0, 0).astype(BF16)
+        cols = pl.ds(pl.multiple_of(place[i] * wide + first, HEAD_DIM), cw)
+        copy = pltpu.make_async_copy(made_ref.at[i], out.at[:, cols], sem.at[i])
+        copy.start()
+        copies.append(copy)
+    for copy in copies:
+        copy.wait()
 
 
 def per_device(n, nd, block_input, cotangent, pool_weight):
@@ -262,13 +267,19 @@
     weight_grad = shares[0]
     for k in range(1, nd):
         weight_grad = weight_grad + send(shares[k], "dp", nd, k)
-    input_grad = pl.pallas_call(
-        functools.partial(spread_kernel, n, nd, wide),
-        out_shape=shape((rows, width), BF16),
-        in_specs=[VMEM] * (1 + len(back)),
-        out_specs=VMEM,
-    )(weights, *back)
-    return input_grad[None], weight_grad
+    input_grad = ()
+    for c in range(chunks):
+        input_grad = (
+            pl.pallas_call(
+                functools.partial(spread_kernel, n, nd, wide, c * cw),
+                out_shape=shape((rows, width), BF16),
+                in_specs=[VMEM] * (1 + n) + [ANY] * len(input_grad),
+                out_specs=ANY,
+                input_output_aliases={1 + n: 0} if input_grad else {},
+                scratch_shapes=[pltpu.VMEM((n, rows, cw), BF16), pltpu.SemaphoreType.DMA((n,))],
+            )(weights, *back[c * n : (c + 1) * n], *input_grad),
+        )
+    return input_grad[0][None], weight_grad
 
 
 def solution(mesh):

time: 93.3 us -> 95.2 us (1.020)
  Pallas kernels: 19.7 us -> 21.1 us
    pallas_call x1 -> x2, Pallas kernels: 3.03 us -> 4.58 us  [per_device(): pl.pallas_call(functools.partial(spread_kernel, n, nd, wide, c * cw), out...]
  transfers between devices with their start and end apart: 34 -> 34, of which waited for: 10 -> 9; matrix products, arithmetic and copies ran while one was open for 1% -> 1% of each run, Pallas kernels for 19% -> 21%
where the time goes in v1:
time: 95.2 us; the launch traced here: 94.7 us
  starting transfers between devices  44.1 us (46%)
  waiting for transfers between devices  24.9 us (26%)
  Pallas kernels  21.1 us (22%)
  local copies, waits for them, and re-layouts  2.16 us (2%)
  other arithmetic  1.38 us (1%)
  between operations  1.03 us (1%)
    ppermute x34, starting transfers between devices, send(): return lax.ppermute(block, axis, [(s, s ^ message) for s in range(n)])  44.1 us
    ppermute x34, waiting for transfers between devices, send(): return lax.ppermute(block, axis, [(s, s ^ message) for s in range(n)])  24.9 us
    pallas_call x2, Pallas kernels, per_device(): pl.pallas_call(functools.partial(block_kernel, n, nd, rc, wide, c * cw),...  8.75 us
    pallas_call x3, Pallas kernels, per_device(): pl.pallas_call(functools.partial(cut_kernel, n, wide, c * cw, which), out...  6.2 us
    pallas_call x2, Pallas kernels, per_device(): pl.pallas_call(functools.partial(spread_kernel, n, nd, wide, c * cw), out...  4.58 us
  transfers between devices with their start and end apart: 34, of which 9 were waited for; matrix products, arithmetic and copies ran while one was open for 1% of the time, Pallas kernels for 21%

profile of v1, /device:TPU:0, one launch (start us, length us, event | category | flops | bytes accessed | tf_op | source)
XLA Modules:
  0.0 94.7 jit_solution(7781379561210499962)
XLA Ops:
  0.6 0.9 reshape.7
  1.5 3.0 %collective-permute-start = (f32[16,1024]{1,0:T(8,128)S(1)}, f32[16,1024]{1,0:T(8,128)S(1)}, u32[]{:S(2)}, u32[]{:S(2)}) collective-permute-start(f32[16,1024]{1,0:T(8,128)S(1)} %reshape.7), channel_id=1, source_target_pairs={{0,1},{1,0},{2,3},{3,2},{4,5},{5,4},{6,7},{7,6},{8,9},{9,8},{10,11... | collective-permute-start | bytes 196616 | tf_op jit(solution)/shard_map/ppermute | solution.py:32
  4.5 1.5 %collective-permute-start.1 = (f32[16,1024]{1,0:T(8,128)S(1)}, f32[16,1024]{1,0:T(8,128)S(1)}, u32[]{:S(2)}, u32[]{:S(2)}) collective-permute-start(f32[16,1024]{1,0:T(8,128)S(1)} %reshape.7), channel_id=1, source_target_pairs={{0,2},{1,3},{2,0},{3,1},{4,6},{5,7},{6,4},{7,5},{8,10},{9,11},{10,... | collective-permute-start | bytes 196616 | tf_op jit(solution)/shard_map/ppermute | solution.py:32
  6.0 2.3 %shard_map.50 = (bf16[256,256]{1,0:T(8,128)(2,1)}, bf16[256,256]{1,0:T(8,128)(2,1)}, bf16[256,256]{1,0:T(8,128)(2,1)}, bf16[256,256]{1,0:T(8,128)(2,1)}, bf16[25...) custom-call(bf16[128,4096]{1,0:T(8,128)(2,1)} %bitcast.11, ...), custom_call_target="tpu_custom_call" | custom-call | tf_op jit(solution)/shard_map/pallas_call | solution.py:221
  8.4 2.7 %collective-permute-start.3 = (bf16[256,256]{1,0:T(8,128)(2,1)}, bf16[256,256]{1,0:T(8,128)(2,1)S(1)}, u32[]{:S(2)}, u32[]{:S(2)}) collective-permute-start(bf16[256,256]{1,0:T(8,128)(2,1)} %get-tuple-element.39), channel_id=1, source_target_pairs={{0,16},{4,20},{8,24},{12,28},{16,0},{20,4},{24,8},{28,12},{1,17},{... | collective-permute-start | bytes 393224 | tf_op jit(solution)/shard_map/ppermute | solution.py:32
  11.0 2.5 %collective-permute-start.5 = (bf16[256,256]{1,0:T(8,128)(2,1)}, bf16[256,256]{1,0:T(8,128)(2,1)S(1)}, u32[]{:S(2)}, u32[]{:S(2)}) collective-permute-start(bf16[256,256]{1,0:T(8,128)(2,1)} %get-tuple-element.41), channel_id=1, source_target_pairs={{0,24},{4,28},{8,16},{12,20},{16,8},{20,12},{24,0},{28,4},{1,25},{... | collective-permute-start | bytes 393224 | tf_op jit(solution)/shard_map/ppermute | solution.py:32
  13.6 0.0 collective-permute-done
  13.6 1.2 %collective-permute-start.6 = (bf16[256,256]{1,0:T(8,128)(2,1)}, bf16[256,256]{1,0:T(8,128)(2,1)S(1)}, u32[]{:S(2)}, u32[]{:S(2)}) collective-permute-start(bf16[256,256]{1,0:T(8,128)(2,1)} %get-tuple-element.42), channel_id=1, source_target_pairs={{0,28},{4,24},{8,20},{12,16},{16,12},{20,8},{24,4},{28,0},{1,29},{... | collective-permute-start | bytes 393224 | tf_op jit(solution)/shard_map/ppermute | solution.py:32
  14.8 0.0 collective-permute-done.1
  14.8 0.5 collective-permute-start.2
  15.3 2.0 %shard_map.53 = (bf16[256,256]{1,0:T(8,128)(2,1)}, bf16[256,256]{1,0:T(8,128)(2,1)}, bf16[256,256]{1,0:T(8,128)(2,1)}, bf16[256,256]{1,0:T(8,128)(2,1)}) custom-call(bf16[128,4096]{1,0:T(8,128)(2,1)} %bitcast.12, bf16[128,4096]{1,0:T(8,128)(2,1)} %bitcast.15), custom_call_target="tpu_custom_call" | custom-call | tf_op jit(solution)/shard_map/pallas_call | solution.py:221
  17.2 2.7 %collective-permute-done.2 = f32[16,1024]{1,0:T(8,128)S(1)} collective-permute-done((f32[16,1024]{1,0:T(8,128)S(1)}, f32[16,1024]{1,0:T(8,128)S(1)}, u32[]{:S(2)}, u32[]{:S(2)}) %collective-permute-start.2) | collective-permute-done | bytes 65568 | tf_op jit(solution)/shard_map/ppermute | solution.py:32
  20.0 0.0 collective-permute-start.7
  20.0 6.7 %collective-permute-done.3.refs_1_ = bf16[256,256]{1,0:T(8,128)(2,1)S(1)} collective-permute-done((bf16[256,256]{1,0:T(8,128)(2,1)}, bf16[256,256]{1,0:T(8,128)(2,1)S(1)}, u32[]{:S(2)}, u32[]{:S(2)}) %collective-permute-start.3) | collective-permute-done | bytes 131104 | tf_op jit(solution)/shard_map/ppermute | solution.py:32
  26.7 0.0 collective-permute-start.8
  26.7 0.6 collective-permute-done.4.refs_2_
  27.3 2.0 %collective-permute-start.9 = (bf16[256,256]{1,0:T(8,128)(2,1)S(1)}, bf16[256,256]{1,0:T(8,128)(2,1)S(1)}, u32[]{:S(2)}, u32[]{:S(2)}) collective-permute-start(bf16[256,256]{1,0:T(8,128)(2,1)S(1)} %copy-done.33), channel_id=1, source_target_pairs={{0,4},{4,0},{8,12},{12,8},{16,20},{20,16},{24,28},{28,24},{1,5},{5... | collective-permute-start | bytes 393224 | tf_op jit(solution)/shard_map/ppermute | solution.py:32
  29.3 4.6 %collective-permute-start.17 = (bf16[256,256]{1,0:T(8,128)(2,1)}, bf16[256,256]{1,0:T(8,128)(2,1)S(1)}, u32[]{:S(2)}, u32[]{:S(2)}) collective-permute-start(bf16[256,256]{1,0:T(8,128)(2,1)} %get-tuple-element.55), channel_id=1, source_target_pairs={{0,16},{4,20},{8,24},{12,28},{16,0},{20,4},{24,8},{28,12},{1,17},{... | collective-permute-start | bytes 393224 | tf_op jit(solution)/shard_map/ppermute | solution.py:32
  33.8 0.0 copy-start
  33.8 2.4 %collective-permute-start.18 = (bf16[256,256]{1,0:T(8,128)(2,1)}, bf16[256,256]{1,0:T(8,128)(2,1)S(1)}, u32[]{:S(2)}, u32[]{:S(2)}) collective-permute-start(bf16[256,256]{1,0:T(8,128)(2,1)} %get-tuple-element.56), channel_id=1, source_target_pairs={{0,20},{4,16},{8,28},{12,24},{16,4},{20,0},{24,12},{28,8},{1,21},{... | collective-permute-start | bytes 393224 | tf_op jit(solution)/shard_map/ppermute | solution.py:32
  36.2 1.9 %shard_map.52 = (bf16[256,256]{1,0:T(8,128)(2,1)}, bf16[256,256]{1,0:T(8,128)(2,1)}, bf16[256,256]{1,0:T(8,128)(2,1)}, bf16[256,256]{1,0:T(8,128)(2,1)}) custom-call(bf16[128,4096]{1,0:T(8,128)(2,1)} %bitcast.13, bf16[128,4096]{1,0:T(8,128)(2,1)} %bitcast.16), custom_call_target="tpu_custom_call" | custom-call | tf_op jit(solution)/shard_map/pallas_call | solution.py:221
  38.2 0.6 collective-permute-start.19
  38.9 0.0 collective-permute-done.8.refs_6_
  38.9 3.1 %collective-permute-start.20 = (bf16[256,256]{1,0:T(8,128)(2,1)S(1)}, bf16[256,256]{1,0:T(8,128)(2,1)S(1)}, u32[]{:S(2)}, u32[]{:S(2)}) collective-permute-start(bf16[256,256]{1,0:T(8,128)(2,1)S(1)} %copy-done.30), channel_id=1, source_target_pairs={{0,28},{4,24},{8,20},{12,16},{16,12},{20,8},{24,4},{28,0},{1,29},{... | collective-permute-start | bytes 393224 | tf_op jit(solution)/shard_map/ppermute | solution.py:32
  41.9 0.0 collective-permute-done.9.refs_7_
  41.9 0.0 collective-permute-start.21
  41.9 7.3 %collective-permute-done.17.refs_1_ = bf16[256,256]{1,0:T(8,128)(2,1)S(1)} collective-permute-done((bf16[256,256]{1,0:T(8,128)(2,1)}, bf16[256,256]{1,0:T(8,128)(2,1)S(1)}, u32[]{:S(2)}, u32[]{:S(2)}) %collective-permute-start.17) | collective-permute-done | bytes 131104 | tf_op jit(solution)/shard_map/ppermute | solution.py:32
  49.2 0.0 collective-permute-start.22
  49.2 2.2 %collective-permute-done.18.refs_2_ = bf16[256,256]{1,0:T(8,128)(2,1)S(1)} collective-permute-done((bf16[256,256]{1,0:T(8,128)(2,1)}, bf16[256,256]{1,0:T(8,128)(2,1)S(1)}, u32[]{:S(2)}, u32[]{:S(2)}) %collective-permute-start.18) | collective-permute-done | bytes 131104 | tf_op jit(solution)/shard_map/ppermute | solution.py:32
  51.4 0.5 collective-permute-start.23
  51.9 0.7 pad_maximum_fusion.weight
  52.7 4.4 %shard_map.51 = (bf16[112,256]{1,0:T(8,128)(2,1)}, bf16[112,256]{1,0:T(8,128)(2,1)}, bf16[112,256]{1,0:T(8,128)(2,1)}, bf16[112,256]{1,0:T(8,128)(2,1)}, bf16[11...) custom-call(f32[4,16,1024]{2,1,0:T(8,128)} %pad_maximum_fusion.weight, ...), custom_call_target="tpu_custom_call" | custom-call | tf_op jit(solution)/shard_map/pallas_call | solution.py:241
  57.0 0.0 collective-permute-done.19.refs_3_
  57.0 0.7 collective-permute-start.10
  57.7 0.0 collective-permute-done.20.refs_4_
  57.7 1.7 %collective-permute-start.11 = (bf16[112,256]{1,0:T(8,128)(2,1)}, bf16[112,256]{1,0:T(8,128)(2,1)S(1)}, u32[]{:S(2)}, u32[]{:S(2)}) collective-permute-start(bf16[112,256]{1,0:T(8,128)(2,1)} %get-tuple-element.48), channel_id=1, source_target_pairs={{0,20},{4,16},{8,28},{12,24},{16,4},{20,0},{24,12},{28,8},{1,21},{... | collective-permute-start | bytes 172040 | tf_op jit(solution)/shard_map/ppermute | solution.py:32
  59.4 0.0 collective-permute-done.21.refs_5_
  59.4 2.9 %collective-permute-start.12 = (bf16[112,256]{1,0:T(8,128)(2,1)}, bf16[112,256]{1,0:T(8,128)(2,1)S(1)}, u32[]{:S(2)}, u32[]{:S(2)}) collective-permute-start(bf16[112,256]{1,0:T(8,128)(2,1)} %get-tuple-element.49), channel_id=1, source_target_pairs={{0,24},{4,28},{8,16},{12,20},{16,8},{20,12},{24,0},{28,4},{1,25},{... | collective-permute-start | bytes 172040 | tf_op jit(solution)/shard_map/ppermute | solution.py:32
  62.3 0.0 collective-permute-done.22.refs_6_
  62.3 1.0 %collective-permute-start.13 = (bf16[112,256]{1,0:T(8,128)(2,1)}, bf16[112,256]{1,0:T(8,128)(2,1)S(1)}, u32[]{:S(2)}, u32[]{:S(2)}) collective-permute-start(bf16[112,256]{1,0:T(8,128)(2,1)} %get-tuple-element.50), channel_id=1, source_target_pairs={{0,28},{4,24},{8,20},{12,16},{16,12},{20,8},{24,4},{28,0},{1,29},{... | collective-permute-start | bytes 172040 | tf_op jit(solution)/shard_map/ppermute | solution.py:32
  63.3 0.0 collective-permute-done.23.refs_7_
  63.3 0.6 copy-done.28
  63.9 4.4 %shard_map.54 = (bf16[112,256]{1,0:T(8,128)(2,1)}, bf16[112,256]{1,0:T(8,128)(2,1)}, bf16[112,256]{1,0:T(8,128)(2,1)}, bf16[112,256]{1,0:T(8,128)(2,1)}, bf16[11...) custom-call(f32[4,16,1024]{2,1,0:T(8,128)} %pad_maximum_fusion.weight, ...), custom_call_target="tpu_custom_call" | custom-call | tf_op jit(solution)/shard_map/pallas_call | solution.py:241
  68.4 0.8 collective-permute-start.15
  69.2 0.8 collective-permute-start.16
  70.1 1.6 %collective-permute-start.24 = (bf16[112,256]{1,0:T(8,128)(2,1)}, bf16[112,256]{1,0:T(8,128)(2,1)S(1)}, u32[]{:S(2)}, u32[]{:S(2)}) collective-permute-start(bf16[112,256]{1,0:T(8,128)(2,1)} %get-tuple-element.63), channel_id=1, source_target_pairs={{0,16},{4,20},{8,24},{12,28},{16,0},{20,4},{24,8},{28,12},{1,17},{... | collective-permute-start | bytes 172040 | tf_op jit(solution)/shard_map/ppermute | solution.py:32
  71.7 0.7 collective-permute-start.25
  72.4 2.5 %collective-permute-start.26 = (bf16[112,256]{1,0:T(8,128)(2,1)}, bf16[112,256]{1,0:T(8,128)(2,1)S(1)}, u32[]{:S(2)}, u32[]{:S(2)}) collective-permute-start(bf16[112,256]{1,0:T(8,128)(2,1)} %get-tuple-element.65), channel_id=1, source_target_pairs={{0,24},{4,28},{8,16},{12,20},{16,8},{20,12},{24,0},{28,4},{1,25},{... | collective-permute-start | bytes 172040 | tf_op jit(solution)/shard_map/ppermute | solution.py:32
  75.0 1.3 %collective-permute-start.27 = (bf16[112,256]{1,0:T(8,128)(2,1)}, bf16[112,256]{1,0:T(8,128)(2,1)S(1)}, u32[]{:S(2)}, u32[]{:S(2)}) collective-permute-start(bf16[112,256]{1,0:T(8,128)(2,1)} %get-tuple-element.66), channel_id=1, source_target_pairs={{0,28},{4,24},{8,20},{12,16},{16,12},{20,8},{24,4},{28,0},{1,29},{... | collective-permute-start | bytes 172040 | tf_op jit(solution)/shard_map/ppermute | solution.py:32
  76.3 3.0 %collective-permute-done.24.refs_1_ = bf16[112,256]{1,0:T(8,128)(2,1)S(1)} collective-permute-done((bf16[112,256]{1,0:T(8,128)(2,1)}, bf16[112,256]{1,0:T(8,128)(2,1)S(1)}, u32[]{:S(2)}, u32[]{:S(2)}) %collective-permute-start.24) | collective-permute-done | bytes 57376 | tf_op jit(solution)/shard_map/ppermute | solution.py:32
  79.2 0.3 collective-permute-done.25.refs_2_
  79.6 1.9 %collective-permute-start.30 = (bf16[112,256]{1,0:T(8,128)(2,1)}, bf16[112,256]{1,0:T(8,128)(2,1)S(1)}, u32[]{:S(2)}, u32[]{:S(2)}) collective-permute-start(bf16[112,256]{1,0:T(8,128)(2,1)} %get-tuple-element.69), channel_id=1, source_target_pairs={{0,4},{4,0},{8,12},{12,8},{16,20},{20,16},{24,28},{28,24},{1,5},{5... | collective-permute-start | bytes 172040 | tf_op jit(solution)/shard_map/ppermute | solution.py:32
  81.5 1.0 %collective-permute-done.28.refs_5_ = bf16[112,256]{1,0:T(8,128)(2,1)S(1)} collective-permute-done((bf16[112,256]{1,0:T(8,128)(2,1)}, bf16[112,256]{1,0:T(8,128)(2,1)S(1)}, u32[]{:S(2)}, u32[]{:S(2)}) %collective-permute-start.28) | collective-permute-done | bytes 57376 | tf_op jit(solution)/shard_map/ppermute | solution.py:32
  82.5 1.2 %collective-permute-done.29.refs_6_ = bf16[112,256]{1,0:T(8,128)(2,1)S(1)} collective-permute-done((bf16[112,256]{1,0:T(8,128)(2,1)}, bf16[112,256]{1,0:T(8,128)(2,1)S(1)}, u32[]{:S(2)}, u32[]{:S(2)}) %collective-permute-start.29) | collective-permute-done | bytes 57376 | tf_op jit(solution)/shard_map/ppermute | solution.py:32
  83.8 0.5 copy-done.6
  84.3 0.0 copy-done.7
  84.3 1.6 %shard_map.57 = (f32[4,4,1024]{2,1,0:T(4,128)}, f32[4,4,1024]{2,1,0:T(4,128)}, f32[4,4,1024]{2,1,0:T(4,128)}, f32[4,4,1024]{2,1,0:T(4,128)}) custom-call(bf16[112,256]{1,0:T(8,128)(2,1)} %get-tuple-element.62.refs_0_, bf16[112,256]{1,0:T(8,128)(2,1)} %copy-done.1, bf16[112,256]{1,0:T(8,128)(2,1)} %copy-done.2, bf16[112,256]{1,0:T(8,128)(2,1)} %copy-done.3, ...), custom_call_target="tpu_custom_call" | custom-call | tf_op jit(solution)/shard_map/pallas_call | solution.py:259
  85.9 0.5 collective-permute-start.33
  86.4 1.5 %collective-permute-start.32 = (f32[4,4,1024]{2,1,0:T(4,128)}, f32[4,4,1024]{2,1,0:T(4,128)S(1)}, u32[]{:S(2)}, u32[]{:S(2)}) collective-permute-start(f32[4,4,1024]{2,1,0:T(4,128)} %get-tuple-element.72), channel_id=1, source_target_pairs={{0,2},{1,3},{2,0},{3,1},{4,6},{5,7},{6,4},{7,5},{8,10},{9,11},{10,... | collective-permute-start | bytes 196616 | tf_op jit(solution)/shard_map/ppermute | solution.py:32
  88.0 1.5 %collective-permute-start.31 = (f32[4,4,1024]{2,1,0:T(4,128)}, f32[4,4,1024]{2,1,0:T(4,128)S(1)}, u32[]{:S(2)}, u32[]{:S(2)}) collective-permute-start(f32[4,4,1024]{2,1,0:T(4,128)} %get-tuple-element.71), channel_id=1, source_target_pairs={{0,1},{1,0},{2,3},{3,2},{4,5},{5,4},{6,7},{7,6},{8,9},{9,8},{10,11... | collective-permute-start | bytes 196616 | tf_op jit(solution)/shard_map/ppermute | solution.py:32
  89.4 2.3 %shard_map.55.refs_8_ = bf16[128,4096]{1,0:T(8,128)(2,1)} custom-call(f32[4,16,1024]{2,1,0:T(8,128)} %pad_maximum_fusion.weight, bf16[112,256]{1,0:T(8,128)(2,1)} %get-tuple-element.62.refs_0_, bf16[112,256]{1,0:T(8,128)(2,1)} %copy-done.1, bf16[112,256]{1,0:T(8,128)(2,1)} %copy-done.2, bf16[112,256]{1,0:T(8,128)(2,1)} %copy-done.3, ...), custom_call_target="tpu_custom_call" | custom-call | tf_op jit(solution)/shard_map/pallas_call | solution.py:273
  91.7 0.0 copy-start.29
  91.7 2.3 %shard_map.56 = bf16[128,4096]{1,0:T(8,128)(2,1)} custom-call(f32[4,16,1024]{2,1,0:T(8,128)} %pad_maximum_fusion.weight, bf16[112,256]{1,0:T(8,128)(2,1)} %get-tuple-element.46.refs_0_.refs_8_, bf16[112,256]{1,0:T(8,128)(2,1)} %copy-done.8, bf16[112,256]{1,0:T(8,128)(2,1)} %copy-done.9, bf16[112,256]{1,0:T(8,128)(2,1)} %copy-done.10, ...), custom_call_target="tpu_custom_call", output_to_operand_aliasing={{}: (9, {})} | custom-call | tf_op jit(solution)/shard_map/pallas_call | solution.py:273
  94.1 0.6 add_add_fusion
  (92 shorter events, 0.2 us)
Async XLA Ops:
  1.5 12.1 %collective-permute-start = (f32[16,1024]{1,0:T(8,128)S(1)}, f32[16,1024]{1,0:T(8,128)S(1)}, u32[]{:S(2)}, u32[]{:S(2)}) collective-permute-start(f32[16,1024]{1,0:T(8,128)S(1)} %reshape.7), channel_id=1, source_target_pairs={{0,1},{1,0},{2,3},{3,2},{4,5},{5,4},{6,7},{7,6},{8,9},{9,8},{10,11... | collective-permute-start | bytes 196616 | tf_op jit(solution)/shard_map/ppermute | solution.py:32
  4.5 10.3 %collective-permute-start.1 = (f32[16,1024]{1,0:T(8,128)S(1)}, f32[16,1024]{1,0:T(8,128)S(1)}, u32[]{:S(2)}, u32[]{:S(2)}) collective-permute-start(f32[16,1024]{1,0:T(8,128)S(1)} %reshape.7), channel_id=1, source_target_pairs={{0,2},{1,3},{2,0},{3,1},{4,6},{5,7},{6,4},{7,5},{8,10},{9,11},{10,... | collective-permute-start | bytes 196616 | tf_op jit(solution)/shard_map/ppermute | solution.py:32
  8.4 18.3 %collective-permute-start.3 = (bf16[256,256]{1,0:T(8,128)(2,1)}, bf16[256,256]{1,0:T(8,128)(2,1)S(1)}, u32[]{:S(2)}, u32[]{:S(2)}) collective-permute-start(bf16[256,256]{1,0:T(8,128)(2,1)} %get-tuple-element.39), channel_id=1, source_target_pairs={{0,16},{4,20},{8,24},{12,28},{16,0},{20,4},{24,8},{28,12},{1,17},{... | collective-permute-start | bytes 393224 | tf_op jit(solution)/shard_map/ppermute | solution.py:32
  11.0 16.2 %collective-permute-start.4 = (bf16[256,256]{1,0:T(8,128)(2,1)}, bf16[256,256]{1,0:T(8,128)(2,1)S(1)}, u32[]{:S(2)}, u32[]{:S(2)}) collective-permute-start(bf16[256,256]{1,0:T(8,128)(2,1)} %get-tuple-element.40), channel_id=1, source_target_pairs={{0,20},{4,16},{8,28},{12,24},{16,4},{20,0},{24,12},{28,8},{1,21},{... | collective-permute-start | bytes 393224 | tf_op jit(solution)/shard_map/ppermute | solution.py:32
  11.0 18.2 %collective-permute-start.5 = (bf16[256,256]{1,0:T(8,128)(2,1)}, bf16[256,256]{1,0:T(8,128)(2,1)S(1)}, u32[]{:S(2)}, u32[]{:S(2)}) collective-permute-start(bf16[256,256]{1,0:T(8,128)(2,1)} %get-tuple-element.41), channel_id=1, source_target_pairs={{0,24},{4,28},{8,16},{12,20},{16,8},{20,12},{24,0},{28,4},{1,25},{... | collective-permute-start | bytes 393224 | tf_op jit(solution)/shard_map/ppermute | solution.py:32
  13.6 6.4 %copy-start.35 = (bf16[256,256]{1,0:T(8,128)(2,1)S(1)}, bf16[256,256]{1,0:T(8,128)(2,1)}, u32[]{:S(2)}) copy-start(bf16[256,256]{1,0:T(8,128)(2,1)} %get-tuple-element.43) | copy-start | bytes 393220
  13.6 13.1 %copy-start.34 = (bf16[256,256]{1,0:T(8,128)(2,1)S(1)}, bf16[256,256]{1,0:T(8,128)(2,1)}, u32[]{:S(2)}) copy-start(bf16[256,256]{1,0:T(8,128)(2,1)} %get-tuple-element.44) | copy-start | bytes 393220
  13.6 13.7 %copy-start.33 = (bf16[256,256]{1,0:T(8,128)(2,1)S(1)}, bf16[256,256]{1,0:T(8,128)(2,1)}, u32[]{:S(2)}) copy-start(bf16[256,256]{1,0:T(8,128)(2,1)} %get-tuple-element.45) | copy-start | bytes 393220
  13.6 20.2 %collective-permute-start.6 = (bf16[256,256]{1,0:T(8,128)(2,1)}, bf16[256,256]{1,0:T(8,128)(2,1)S(1)}, u32[]{:S(2)}, u32[]{:S(2)}) collective-permute-start(bf16[256,256]{1,0:T(8,128)(2,1)} %get-tuple-element.42), channel_id=1, source_target_pairs={{0,28},{4,24},{8,20},{12,16},{16,12},{20,8},{24,4},{28,0},{1,29},{... | collective-permute-start | bytes 393224 | tf_op jit(solution)/shard_map/ppermute | solution.py:32
  14.8 5.2 %collective-permute-start.2 = (f32[16,1024]{1,0:T(8,128)S(1)}, f32[16,1024]{1,0:T(8,128)S(1)}, u32[]{:S(2)}, u32[]{:S(2)}) collective-permute-start(f32[16,1024]{1,0:T(8,128)S(1)} %reshape.7), channel_id=1, source_target_pairs={{0,3},{1,2},{2,1},{3,0},{4,7},{5,6},{6,5},{7,4},{8,11},{9,10},{10,... | collective-permute-start | bytes 196616 | tf_op jit(solution)/shard_map/ppermute | solution.py:32
  20.0 18.2 %collective-permute-start.7 = (bf16[256,256]{1,0:T(8,128)(2,1)S(1)}, bf16[256,256]{1,0:T(8,128)(2,1)S(1)}, u32[]{:S(2)}, u32[]{:S(2)}) collective-permute-start(bf16[256,256]{1,0:T(8,128)(2,1)S(1)} %copy-done.35), channel_id=1, source_target_pairs={{0,8},{4,12},{8,0},{12,4},{16,24},{20,28},{24,16},{28,20},{1,9},{5... | collective-permute-start | bytes 393224 | tf_op jit(solution)/shard_map/ppermute | solution.py:32
  26.7 11.5 %copy-start.15 = (bf16[256,256]{1,0:T(8,128)(2,1)}, bf16[256,256]{1,0:T(8,128)(2,1)S(1)}, u32[]{:S(2)}) copy-start(bf16[256,256]{1,0:T(8,128)(2,1)S(1)} %collective-permute-done.3.refs_1_) | copy-start | bytes 393220
  26.7 12.2 %collective-permute-start.8 = (bf16[256,256]{1,0:T(8,128)(2,1)S(1)}, bf16[256,256]{1,0:T(8,128)(2,1)S(1)}, u32[]{:S(2)}, u32[]{:S(2)}) collective-permute-start(bf16[256,256]{1,0:T(8,128)(2,1)S(1)} %copy-done.34), channel_id=1, source_target_pairs={{0,12},{4,8},{8,4},{12,0},{16,28},{20,24},{24,20},{28,16},{1,13},{... | collective-permute-start | bytes 393224 | tf_op jit(solution)/shard_map/ppermute | solution.py:32
  27.3 10.9 %copy-start.17 = (bf16[256,256]{1,0:T(8,128)(2,1)}, bf16[256,256]{1,0:T(8,128)(2,1)S(1)}, u32[]{:S(2)}) copy-start(bf16[256,256]{1,0:T(8,128)(2,1)S(1)} %collective-permute-done.4.refs_2_) | copy-start | bytes 393220
  27.3 14.6 %collective-permute-start.9 = (bf16[256,256]{1,0:T(8,128)(2,1)S(1)}, bf16[256,256]{1,0:T(8,128)(2,1)S(1)}, u32[]{:S(2)}, u32[]{:S(2)}) collective-permute-start(bf16[256,256]{1,0:T(8,128)(2,1)S(1)} %copy-done.33), channel_id=1, source_target_pairs={{0,4},{4,0},{8,12},{12,8},{16,20},{20,16},{24,28},{28,24},{1,5},{5... | collective-permute-start | bytes 393224 | tf_op jit(solution)/shard_map/ppermute | solution.py:32
  29.3 8.9 %copy-start.18 = (bf16[256,256]{1,0:T(8,128)(2,1)}, bf16[256,256]{1,0:T(8,128)(2,1)S(1)}, u32[]{:S(2)}) copy-start(bf16[256,256]{1,0:T(8,128)(2,1)S(1)} %collective-permute-done.5.refs_3_) | copy-start | bytes 393220
  29.3 19.9 %collective-permute-start.17 = (bf16[256,256]{1,0:T(8,128)(2,1)}, bf16[256,256]{1,0:T(8,128)(2,1)S(1)}, u32[]{:S(2)}, u32[]{:S(2)}) collective-permute-start(bf16[256,256]{1,0:T(8,128)(2,1)} %get-tuple-element.55), channel_id=1, source_target_pairs={{0,16},{4,20},{8,24},{12,28},{16,0},{20,4},{24,8},{28,12},{1,17},{... | collective-permute-start | bytes 393224 | tf_op jit(solution)/shard_map/ppermute | solution.py:32
  33.8 4.4 %copy-start.20 = (bf16[256,256]{1,0:T(8,128)(2,1)}, bf16[256,256]{1,0:T(8,128)(2,1)S(1)}, u32[]{:S(2)}) copy-start(bf16[256,256]{1,0:T(8,128)(2,1)S(1)} %collective-permute-done.6.refs_4_) | copy-start | bytes 393220
  33.8 4.4 %copy-start.31 = (bf16[256,256]{1,0:T(8,128)(2,1)S(1)}, bf16[256,256]{1,0:T(8,128)(2,1)}, u32[]{:S(2)}) copy-start(bf16[256,256]{1,0:T(8,128)(2,1)} %get-tuple-element.57) | copy-start | bytes 393220
  33.8 5.0 %copy-start.30 = (bf16[256,256]{1,0:T(8,128)(2,1)S(1)}, bf16[256,256]{1,0:T(8,128)(2,1)}, u32[]{:S(2)}) copy-start(bf16[256,256]{1,0:T(8,128)(2,1)} %get-tuple-element.58) | copy-start | bytes 393220
  33.8 15.4 %copy-start = (f32[4,4,1024]{2,1,0:T(4,128)S(1)}, f32[4,4,1024]{2,1,0:T(4,128)}, u32[]{:S(2)}) copy-start(f32[4,4,1024]{2,1,0:T(4,128)} %param.5) | copy-start | bytes 196612
  33.8 17.5 %collective-permute-start.18 = (bf16[256,256]{1,0:T(8,128)(2,1)}, bf16[256,256]{1,0:T(8,128)(2,1)S(1)}, u32[]{:S(2)}, u32[]{:S(2)}) collective-permute-start(bf16[256,256]{1,0:T(8,128)(2,1)} %get-tuple-element.56), channel_id=1, source_target_pairs={{0,20},{4,16},{8,28},{12,24},{16,4},{20,0},{24,12},{28,8},{1,21},{... | collective-permute-start | bytes 393224 | tf_op jit(solution)/shard_map/ppermute | solution.py:32
  38.2 13.2 %copy-start.32 = (bf16[256,256]{1,0:T(8,128)(2,1)S(1)}, bf16[256,256]{1,0:T(8,128)(2,1)}, u32[]{:S(2)}) copy-start(bf16[256,256]{1,0:T(8,128)(2,1)} %get-tuple-element.61) | copy-start | bytes 393220
  38.2 14.4 %copy-start.23 = (bf16[256,256]{1,0:T(8,128)(2,1)}, bf16[256,256]{1,0:T(8,128)(2,1)S(1)}, u32[]{:S(2)}) copy-start(bf16[256,256]{1,0:T(8,128)(2,1)S(1)} %collective-permute-done.7.refs_5_) | copy-start | bytes 393220
  38.2 18.8 %collective-permute-start.19 = (bf16[256,256]{1,0:T(8,128)(2,1)S(1)}, bf16[256,256]{1,0:T(8,128)(2,1)S(1)}, u32[]{:S(2)}, u32[]{:S(2)}) collective-permute-start(bf16[256,256]{1,0:T(8,128)(2,1)S(1)} %copy-done.31), channel_id=1, source_target_pairs={{0,24},{4,28},{8,16},{12,20},{16,8},{20,12},{24,0},{28,4},{1,25},{... | collective-permute-start | bytes 393224 | tf_op jit(solution)/shard_map/ppermute | solution.py:32
  38.9 13.8 %copy-start.25 = (bf16[256,256]{1,0:T(8,128)(2,1)}, bf16[256,256]{1,0:T(8,128)(2,1)S(1)}, u32[]{:S(2)}) copy-start(bf16[256,256]{1,0:T(8,128)(2,1)S(1)} %collective-permute-done.8.refs_6_) | copy-start | bytes 393220
  38.9 18.8 %collective-permute-start.20 = (bf16[256,256]{1,0:T(8,128)(2,1)S(1)}, bf16[256,256]{1,0:T(8,128)(2,1)S(1)}, u32[]{:S(2)}, u32[]{:S(2)}) collective-permute-start(bf16[256,256]{1,0:T(8,128)(2,1)S(1)} %copy-done.30), channel_id=1, source_target_pairs={{0,28},{4,24},{8,20},{12,16},{16,12},{20,8},{24,4},{28,0},{1,29},{... | collective-permute-start | bytes 393224 | tf_op jit(solution)/shard_map/ppermute | solution.py:32
  41.9 10.7 %copy-start.27 = (bf16[256,256]{1,0:T(8,128)(2,1)}, bf16[256,256]{1,0:T(8,128)(2,1)S(1)}, u32[]{:S(2)}) copy-start(bf16[256,256]{1,0:T(8,128)(2,1)S(1)} %collective-permute-done.9.refs_7_) | copy-start | bytes 393220
  41.9 17.4 %collective-permute-start.21 = (bf16[256,256]{1,0:T(8,128)(2,1)}, bf16[256,256]{1,0:T(8,128)(2,1)S(1)}, u32[]{:S(2)}, u32[]{:S(2)}) collective-permute-start(bf16[256,256]{1,0:T(8,128)(2,1)} %get-tuple-element.59), channel_id=1, source_target_pairs={{0,8},{4,12},{8,0},{12,4},{16,24},{20,28},{24,16},{28,20},{1,9},{5... | collective-permute-start | bytes 393224 | tf_op jit(solution)/shard_map/ppermute | solution.py:32
  49.2 3.4 %copy-start.16 = (bf16[256,256]{1,0:T(8,128)(2,1)}, bf16[256,256]{1,0:T(8,128)(2,1)S(1)}, u32[]{:S(2)}) copy-start(bf16[256,256]{1,0:T(8,128)(2,1)S(1)} %collective-permute-done.17.refs_1_) | copy-start | bytes 393220
  49.2 13.1 %collective-permute-start.22 = (bf16[256,256]{1,0:T(8,128)(2,1)}, bf16[256,256]{1,0:T(8,128)(2,1)S(1)}, u32[]{:S(2)}, u32[]{:S(2)}) collective-permute-start(bf16[256,256]{1,0:T(8,128)(2,1)} %get-tuple-element.60), channel_id=1, source_target_pairs={{0,12},{4,8},{8,4},{12,0},{16,28},{20,24},{24,20},{28,16},{1,13},{... | collective-permute-start | bytes 393224 | tf_op jit(solution)/shard_map/ppermute | solution.py:32
  51.4 11.9 %collective-permute-start.23 = (bf16[256,256]{1,0:T(8,128)(2,1)S(1)}, bf16[256,256]{1,0:T(8,128)(2,1)S(1)}, u32[]{:S(2)}, u32[]{:S(2)}) collective-permute-start(bf16[256,256]{1,0:T(8,128)(2,1)S(1)} %copy-done.32), channel_id=1, source_target_pairs={{0,4},{4,0},{8,12},{12,8},{16,20},{20,16},{24,28},{28,24},{1,5},{5... | collective-permute-start | bytes 393224 | tf_op jit(solution)/shard_map/ppermute | solution.py:32
  57.0 6.3 %copy-start.21 = (bf16[256,256]{1,0:T(8,128)(2,1)}, bf16[256,256]{1,0:T(8,128)(2,1)S(1)}, u32[]{:S(2)}) copy-start(bf16[256,256]{1,0:T(8,128)(2,1)S(1)} %collective-permute-done.19.refs_3_) | copy-start | bytes 393220
  57.0 11.3 %collective-permute-start.10 = (bf16[112,256]{1,0:T(8,128)(2,1)}, bf16[112,256]{1,0:T(8,128)(2,1)S(1)}, u32[]{:S(2)}, u32[]{:S(2)}) collective-permute-start(bf16[112,256]{1,0:T(8,128)(2,1)} %get-tuple-element.47), channel_id=1, source_target_pairs={{0,16},{4,20},{8,24},{12,28},{16,0},{20,4},{24,8},{28,12},{1,17},{... | collective-permute-start | bytes 172040 | tf_op jit(solution)/shard_map/ppermute | solution.py:32
  57.7 5.6 %copy-start.22 = (bf16[256,256]{1,0:T(8,128)(2,1)}, bf16[256,256]{1,0:T(8,128)(2,1)S(1)}, u32[]{:S(2)}) copy-start(bf16[256,256]{1,0:T(8,128)(2,1)S(1)} %collective-permute-done.20.refs_4_) | copy-start | bytes 393220
  57.7 11.5 %collective-permute-start.11 = (bf16[112,256]{1,0:T(8,128)(2,1)}, bf16[112,256]{1,0:T(8,128)(2,1)S(1)}, u32[]{:S(2)}, u32[]{:S(2)}) collective-permute-start(bf16[112,256]{1,0:T(8,128)(2,1)} %get-tuple-element.48), channel_id=1, source_target_pairs={{0,20},{4,16},{8,28},{12,24},{16,4},{20,0},{24,12},{28,8},{1,21},{... | collective-permute-start | bytes 172040 | tf_op jit(solution)/shard_map/ppermute | solution.py:32
  59.4 4.0 %copy-start.24 = (bf16[256,256]{1,0:T(8,128)(2,1)}, bf16[256,256]{1,0:T(8,128)(2,1)S(1)}, u32[]{:S(2)}) copy-start(bf16[256,256]{1,0:T(8,128)(2,1)S(1)} %collective-permute-done.21.refs_5_) | copy-start | bytes 393220
  59.4 10.7 %collective-permute-start.12 = (bf16[112,256]{1,0:T(8,128)(2,1)}, bf16[112,256]{1,0:T(8,128)(2,1)S(1)}, u32[]{:S(2)}, u32[]{:S(2)}) collective-permute-start(bf16[112,256]{1,0:T(8,128)(2,1)} %get-tuple-element.49), channel_id=1, source_target_pairs={{0,24},{4,28},{8,16},{12,20},{16,8},{20,12},{24,0},{28,4},{1,25},{... | collective-permute-start | bytes 172040 | tf_op jit(solution)/shard_map/ppermute | solution.py:32
  62.3 9.4 %collective-permute-start.13 = (bf16[112,256]{1,0:T(8,128)(2,1)}, bf16[112,256]{1,0:T(8,128)(2,1)S(1)}, u32[]{:S(2)}, u32[]{:S(2)}) collective-permute-start(bf16[112,256]{1,0:T(8,128)(2,1)} %get-tuple-element.50), channel_id=1, source_target_pairs={{0,28},{4,24},{8,20},{12,16},{16,12},{20,8},{24,4},{28,0},{1,29},{... | collective-permute-start | bytes 172040 | tf_op jit(solution)/shard_map/ppermute | solution.py:32
  63.3 9.1 %collective-permute-start.14 = (bf16[112,256]{1,0:T(8,128)(2,1)}, bf16[112,256]{1,0:T(8,128)(2,1)S(1)}, u32[]{:S(2)}, u32[]{:S(2)}) collective-permute-start(bf16[112,256]{1,0:T(8,128)(2,1)} %get-tuple-element.51), channel_id=1, source_target_pairs={{0,8},{4,12},{8,0},{12,4},{16,24},{20,28},{24,16},{28,20},{1,9},{5... | collective-permute-start | bytes 172040 | tf_op jit(solution)/shard_map/ppermute | solution.py:32
  63.9 4.4 %copy-start.37 = (bf16[112,256]{1,0:T(8,128)(2,1)S(1)}, bf16[112,256]{1,0:T(8,128)(2,1)}, u32[]{:S(2)}) copy-start(bf16[112,256]{1,0:T(8,128)(2,1)} %get-tuple-element.52) | copy-start | bytes 172036
  63.9 5.3 %copy-start.36 = (bf16[112,256]{1,0:T(8,128)(2,1)S(1)}, bf16[112,256]{1,0:T(8,128)(2,1)}, u32[]{:S(2)}) copy-start(bf16[112,256]{1,0:T(8,128)(2,1)} %get-tuple-element.53) | copy-start | bytes 172036
  68.3 15.3 %copy-start.8 = (bf16[112,256]{1,0:T(8,128)(2,1)}, bf16[112,256]{1,0:T(8,128)(2,1)S(1)}, u32[]{:S(2)}) copy-start(bf16[112,256]{1,0:T(8,128)(2,1)S(1)} %collective-permute-done.10.refs_1_.refs_9_) | copy-start | bytes 172036
  68.4 6.6 %collective-permute-start.15 = (bf16[112,256]{1,0:T(8,128)(2,1)S(1)}, bf16[112,256]{1,0:T(8,128)(2,1)S(1)}, u32[]{:S(2)}, u32[]{:S(2)}) collective-permute-start(bf16[112,256]{1,0:T(8,128)(2,1)S(1)} %copy-done.37), channel_id=1, source_target_pairs={{0,12},{4,8},{8,4},{12,0},{16,28},{20,24},{24,20},{28,16},{1,13},{... | collective-permute-start | bytes 172040 | tf_op jit(solution)/shard_map/ppermute | solution.py:32
  69.2 14.5 %copy-start.9 = (bf16[112,256]{1,0:T(8,128)(2,1)}, bf16[112,256]{1,0:T(8,128)(2,1)S(1)}, u32[]{:S(2)}) copy-start(bf16[112,256]{1,0:T(8,128)(2,1)S(1)} %collective-permute-done.11.refs_2_.refs_10_) | copy-start | bytes 172036
  69.2 7.0 %collective-permute-start.16 = (bf16[112,256]{1,0:T(8,128)(2,1)S(1)}, bf16[112,256]{1,0:T(8,128)(2,1)S(1)}, u32[]{:S(2)}, u32[]{:S(2)}) collective-permute-start(bf16[112,256]{1,0:T(8,128)(2,1)S(1)} %copy-done.36), channel_id=1, source_target_pairs={{0,4},{4,0},{8,12},{12,8},{16,20},{20,16},{24,28},{28,24},{1,5},{5... | collective-permute-start | bytes 172040 | tf_op jit(solution)/shard_map/ppermute | solution.py:32
  70.1 13.6 %copy-start.10 = (bf16[112,256]{1,0:T(8,128)(2,1)}, bf16[112,256]{1,0:T(8,128)(2,1)S(1)}, u32[]{:S(2)}) copy-start(bf16[112,256]{1,0:T(8,128)(2,1)S(1)} %collective-permute-done.12.refs_3_.refs_11_) | copy-start | bytes 172036
  70.1 9.2 %collective-permute-start.24 = (bf16[112,256]{1,0:T(8,128)(2,1)}, bf16[112,256]{1,0:T(8,128)(2,1)S(1)}, u32[]{:S(2)}, u32[]{:S(2)}) collective-permute-start(bf16[112,256]{1,0:T(8,128)(2,1)} %get-tuple-element.63), channel_id=1, source_target_pairs={{0,16},{4,20},{8,24},{12,28},{16,0},{20,4},{24,8},{28,12},{1,17},{... | collective-permute-start | bytes 172040 | tf_op jit(solution)/shard_map/ppermute | solution.py:32
  71.7 12.0 %copy-start.11 = (bf16[112,256]{1,0:T(8,128)(2,1)}, bf16[112,256]{1,0:T(8,128)(2,1)S(1)}, u32[]{:S(2)}) copy-start(bf16[112,256]{1,0:T(8,128)(2,1)S(1)} %collective-permute-done.13.refs_4_.refs_12_) | copy-start | bytes 172036
  71.7 7.9 %collective-permute-start.25 = (bf16[112,256]{1,0:T(8,128)(2,1)}, bf16[112,256]{1,0:T(8,128)(2,1)S(1)}, u32[]{:S(2)}, u32[]{:S(2)}) collective-permute-start(bf16[112,256]{1,0:T(8,128)(2,1)} %get-tuple-element.64), channel_id=1, source_target_pairs={{0,20},{4,16},{8,28},{12,24},{16,4},{20,0},{24,12},{28,8},{1,21},{... | collective-permute-start | bytes 172040 | tf_op jit(solution)/shard_map/ppermute | solution.py:32
  72.4 11.3 %copy-start.12 = (bf16[112,256]{1,0:T(8,128)(2,1)}, bf16[112,256]{1,0:T(8,128)(2,1)S(1)}, u32[]{:S(2)}) copy-start(bf16[112,256]{1,0:T(8,128)(2,1)S(1)} %collective-permute-done.14.refs_5_.refs_13_) | copy-start | bytes 172036
  72.4 9.1 %collective-permute-start.26 = (bf16[112,256]{1,0:T(8,128)(2,1)}, bf16[112,256]{1,0:T(8,128)(2,1)S(1)}, u32[]{:S(2)}, u32[]{:S(2)}) collective-permute-start(bf16[112,256]{1,0:T(8,128)(2,1)} %get-tuple-element.65), channel_id=1, source_target_pairs={{0,24},{4,28},{8,16},{12,20},{16,8},{20,12},{24,0},{28,4},{1,25},{... | collective-permute-start | bytes 172040 | tf_op jit(solution)/shard_map/ppermute | solution.py:32
  75.0 8.8 %copy-start.13 = (bf16[112,256]{1,0:T(8,128)(2,1)}, bf16[112,256]{1,0:T(8,128)(2,1)S(1)}, u32[]{:S(2)}) copy-start(bf16[112,256]{1,0:T(8,128)(2,1)S(1)} %collective-permute-done.15.refs_6_.refs_14_) | copy-start | bytes 172036
  75.0 6.5 %collective-permute-start.27 = (bf16[112,256]{1,0:T(8,128)(2,1)}, bf16[112,256]{1,0:T(8,128)(2,1)S(1)}, u32[]{:S(2)}, u32[]{:S(2)}) collective-permute-start(bf16[112,256]{1,0:T(8,128)(2,1)} %get-tuple-element.66), channel_id=1, source_target_pairs={{0,28},{4,24},{8,20},{12,16},{16,12},{20,8},{24,4},{28,0},{1,29},{... | collective-permute-start | bytes 172040 | tf_op jit(solution)/shard_map/ppermute | solution.py:32
  76.3 7.5 %copy-start.14 = (bf16[112,256]{1,0:T(8,128)(2,1)}, bf16[112,256]{1,0:T(8,128)(2,1)S(1)}, u32[]{:S(2)}) copy-start(bf16[112,256]{1,0:T(8,128)(2,1)S(1)} %collective-permute-done.16.refs_7_.refs_15_) | copy-start | bytes 172036
  76.3 6.2 %collective-permute-start.28 = (bf16[112,256]{1,0:T(8,128)(2,1)}, bf16[112,256]{1,0:T(8,128)(2,1)S(1)}, u32[]{:S(2)}, u32[]{:S(2)}) collective-permute-start(bf16[112,256]{1,0:T(8,128)(2,1)} %get-tuple-element.67), channel_id=1, source_target_pairs={{0,8},{4,12},{8,0},{12,4},{16,24},{20,28},{24,16},{28,20},{1,9},{5... | collective-permute-start | bytes 172040 | tf_op jit(solution)/shard_map/ppermute | solution.py:32
  79.2 4.5 %copy-start.1 = (bf16[112,256]{1,0:T(8,128)(2,1)}, bf16[112,256]{1,0:T(8,128)(2,1)S(1)}, u32[]{:S(2)}) copy-start(bf16[112,256]{1,0:T(8,128)(2,1)S(1)} %collective-permute-done.24.refs_1_) | copy-start | bytes 172036
  79.2 4.4 %collective-permute-start.29 = (bf16[112,256]{1,0:T(8,128)(2,1)}, bf16[112,256]{1,0:T(8,128)(2,1)S(1)}, u32[]{:S(2)}, u32[]{:S(2)}) collective-permute-start(bf16[112,256]{1,0:T(8,128)(2,1)} %get-tuple-element.68), channel_id=1, source_target_pairs={{0,12},{4,8},{8,4},{12,0},{16,28},{20,24},{24,20},{28,16},{1,13},{... | collective-permute-start | bytes 172040 | tf_op jit(solution)/shard_map/ppermute | solution.py:32
  79.6 4.2 %copy-start.2 = (bf16[112,256]{1,0:T(8,128)(2,1)}, bf16[112,256]{1,0:T(8,128)(2,1)S(1)}, u32[]{:S(2)}) copy-start(bf16[112,256]{1,0:T(8,128)(2,1)S(1)} %collective-permute-done.25.refs_2_) | copy-start | bytes 172036
  79.6 4.1 %collective-permute-start.30 = (bf16[112,256]{1,0:T(8,128)(2,1)}, bf16[112,256]{1,0:T(8,128)(2,1)S(1)}, u32[]{:S(2)}, u32[]{:S(2)}) collective-permute-start(bf16[112,256]{1,0:T(8,128)(2,1)} %get-tuple-element.69), channel_id=1, source_target_pairs={{0,4},{4,0},{8,12},{12,8},{16,20},{20,16},{24,28},{28,24},{1,5},{5... | collective-permute-start | bytes 172040 | tf_op jit(solution)/shard_map/ppermute | solution.py:32
  85.9 8.1 %collective-permute-start.33 = (f32[4,4,1024]{2,1,0:T(4,128)}, f32[4,4,1024]{2,1,0:T(4,128)S(1)}, u32[]{:S(2)}, u32[]{:S(2)}) collective-permute-start(f32[4,4,1024]{2,1,0:T(4,128)} %get-tuple-element.73), channel_id=1, source_target_pairs={{0,3},{1,2},{2,1},{3,0},{4,7},{5,6},{6,5},{7,4},{8,11},{9,10},{10,... | collective-permute-start | bytes 196616 | tf_op jit(solution)/shard_map/ppermute | solution.py:32
  86.4 7.6 %collective-permute-start.32 = (f32[4,4,1024]{2,1,0:T(4,128)}, f32[4,4,1024]{2,1,0:T(4,128)S(1)}, u32[]{:S(2)}, u32[]{:S(2)}) collective-permute-start(f32[4,4,1024]{2,1,0:T(4,128)} %get-tuple-element.72), channel_id=1, source_target_pairs={{0,2},{1,3},{2,0},{3,1},{4,6},{5,7},{6,4},{7,5},{8,10},{9,11},{10,... | collective-permute-start | bytes 196616 | tf_op jit(solution)/shard_map/ppermute | solution.py:32
  88.0 6.1 %collective-permute-start.31 = (f32[4,4,1024]{2,1,0:T(4,128)}, f32[4,4,1024]{2,1,0:T(4,128)S(1)}, u32[]{:S(2)}, u32[]{:S(2)}) collective-permute-start(f32[4,4,1024]{2,1,0:T(4,128)} %get-tuple-element.71), channel_id=1, source_target_pairs={{0,1},{1,0},{2,3},{3,2},{4,5},{5,4},{6,7},{7,6},{8,9},{9,8},{10,11... | collective-permute-start | bytes 196616 | tf_op jit(solution)/shard_map/ppermute | solution.py:32
  91.7 2.4 %copy-start.29 = (f32[4,4,1024]{2,1,0:T(4,128)S(1)}, f32[4,4,1024]{2,1,0:T(4,128)}, u32[]{:S(2)}) copy-start(f32[4,4,1024]{2,1,0:T(4,128)} %get-tuple-element.70) | copy-start | bytes 196612
  (8 other events, 10.1 us)
